TPU v7x, 128 devices: a whole 4x4x4 slice. The times are simulated.
128 devices in a mesh: tm: 16 (over z, y), col: 8 (over x, core).
Axes of the slice: x: 4, y: 4, z: 4, core: 2. Of those that a mesh axis runs over, the one named last changes fastest.
Arguments:
- block_values: bfloat16 [8, 32768, 128], P('col', 'tm'), may hold values from -6 to 6
- block_shifts: bfloat16 [8, 32768, 128], P('col', 'tm'), may hold values from -1 to 1
- block_sensor: int32 [8, 32768], P('col', 'tm'), may hold values from 0 to 2047
- block_window: int32 [8, 32768], P('col', 'tm'), may hold values from 0 to 3
- block_owner: int32 [8, 32768, 1], P('col', 'tm'), may hold values from 0 to 15; in each aligned block of 2048 rows (0 to 2047, 2048 to 4095, ..., all dimensions but the last counted through in order) at most 192 rows name the same one
- block_counts: int32 [8, 16], P('col', 'tm'), may hold values from 1536 to 2048
- calibration: bfloat16 [16384, 4096], P('tm', 'col'), may hold values from -0.046875 to 0.046875
Outputs:
- calibrated: bfloat16 [8192, 4096], P('tm', 'col')
Inputs may be any that keep to these rules, and one draw needn't show every extreme that they name: `block_owner`: among the 2048 block slots of one device, at most 192 name the same owner, a bound that some block reaches. The live blocks of device (tm t, col c) are its first block_counts[c, t] slots.
All inputs are finite; a program needn't handle non-finite values.
Results may differ from a plain program's by a relative error of at most 0.015.
Values may be sent and summed in bfloat16 or wider, within the bound.
A program may use at most 128 MiB of HBM per device.

v0:
```python
import jax
import jax.numpy as jnp
from jax import lax
from jax.sharding import Mesh
from jax.sharding import PartitionSpec as P

SENSORS = 16384
ROWS_DEV = 512
TM = ("tm_0", "tm_1")


def cut_rows(length, count):
    unit = 8 if length >= 8 * count else 1
    return [length // unit * k // count * unit for k in range(1, count)]


def gather_in_order(shard, axes, sequence):
    parts = shard[None]
    for k in sequence:
        parts = lax.all_gather(parts, axes[k], axis=0, tiled=True)
    carried = [lax.axis_size(axes[k]) for k in reversed(sequence)]
    parts = parts.reshape(*carried, *shard.shape)
    turned = sorted(range(len(sequence)), key=lambda place: sequence[len(sequence) - 1 - place])
    return parts.transpose(*turned, *range(len(sequence), parts.ndim)).reshape(-1, *shard.shape)


def joined_along(parts, dim):
    lengths = list(parts.shape[1:])
    lengths[dim] *= parts.shape[0]
    return jnp.moveaxis(parts, 0, dim).reshape(lengths)


def gather_all_axes(shard, axes, dim):
    numbers = list(range(len(axes)))[::-1]
    cut = shard.shape.index(max(shard.shape[:-1] or shard.shape))
    edges = [0, *cut_rows(shard.shape[cut], len(axes)), shard.shape[cut]]
    outs = []
    for k, (start, end) in enumerate(zip(edges, edges[1:])):
        if end > start:
            slab = lax.slice_in_dim(shard, start, end, axis=cut)
            outs.append(gather_in_order(slab, axes, numbers[k:] + numbers[:k]))
    return joined_along(jnp.concatenate(outs, axis=cut + 1), dim)


def spread_samples(values, shifts):
    samples = values.astype(jnp.float32)
    offsets = shifts.astype(jnp.float32)
    result = jnp.zeros(samples.shape, jnp.float32)
    lead = [(0, 0)] * (samples.ndim - 1)
    for displace in (-1, 0, 1):
        weight = jnp.maximum(0.0, 1.0 - jnp.abs(offsets - displace)).astype(jnp.bfloat16)
        weight = lax.optimization_barrier(weight).astype(jnp.float32)
        product = weight * samples
        if displace == 1:
            result = result + jnp.pad(product[..., :-1], lead + [(1, 0)])
        elif displace == -1:
            result = jnp.pad(product[..., 1:], lead + [(0, 1)])
        else:
            result = result + product
    return result


def spread_slots(moved_slots):
    return spread_samples(moved_slots[:, :, 0], moved_slots[:, :, 1])


def per_device(
    block_values, block_shifts, block_sensor, block_window, block_owner, block_counts, calibration
):
    values = block_values[0]
    shifts = block_shifts[0]
    blocks = values.shape[0]
    length = values.shape[1]
    owners = lax.axis_size(TM)
    group_size = SENSORS // lax.axis_size("col")
    windows = ROWS_DEV // length
    capacity = blocks * 3 // (2 * owners)
    slot_total = owners * capacity
    block_index = lax.iota(jnp.int32, blocks)
    is_live = block_index < block_counts[0, 0]
    values = jnp.where(is_live[:, None], values, jnp.zeros_like(values))
    owner_ids = block_owner[0, :, 0]
    owner_onehot = (owner_ids[:, None] == lax.iota(jnp.int32, owners)[None, :]).astype(jnp.bfloat16)
    lower_mask = (block_index[:, None] > block_index[None, :]).astype(jnp.bfloat16)
    earlier = jnp.dot(lower_mask, owner_onehot, preferred_element_type=jnp.float32)
    slot_rank = jnp.sum(earlier * owner_onehot.astype(jnp.float32), axis=1).astype(jnp.int32)
    slot_index = owner_ids * capacity + slot_rank
    slot_match = slot_index[None, :] == lax.iota(jnp.int32, slot_total)[:, None]
    source = jnp.max(jnp.where(slot_match, block_index[None, :], -1), axis=1)
    filled = source >= 0
    source_row = jnp.maximum(source, 0)
    row_keys = block_window[0] * group_size + block_sensor[0]
    payload = jnp.stack((values, shifts), axis=1)
    outgoing = jnp.where(
        filled[:, None, None], jnp.take(payload, source_row, axis=0), jnp.zeros((), jnp.bfloat16)
    )
    outgoing = outgoing.reshape(owners, capacity, 2, length)
    outgoing_keys = jnp.where(filled, jnp.take(row_keys, source_row, axis=0), 0).reshape(
        owners, capacity
    )
    contribution = spread_slots(
        lax.all_to_all(outgoing, TM, split_axis=0, concat_axis=0, tiled=True)
    )
    incoming_keys = lax.all_to_all(outgoing_keys, TM, split_axis=0, concat_axis=0, tiled=True)
    flat_keys = incoming_keys.reshape(-1)
    flat_contrib = contribution.reshape(-1, length)
    upper_part = flat_contrib.astype(jnp.bfloat16)
    lower_part = (flat_contrib - upper_part.astype(jnp.float32)).astype(jnp.bfloat16)
    sensor_iota = lax.iota(jnp.int32, group_size)
    window_rows = []
    for window in range(windows):
        target = flat_keys - window * group_size
        place_onehot = (target[:, None] == sensor_iota[None, :]).astype(jnp.bfloat16)
        dims = (((0,), (0,)), ((), ()))
        window_sum = lax.dot_general(
            upper_part, place_onehot, dims, preferred_element_type=jnp.float32
        )
        window_sum = window_sum + lax.dot_general(
            lower_part, place_onehot, dims, preferred_element_type=jnp.float32
        )
        window_rows.append(window_sum)
    aligned = jnp.concatenate(window_rows, axis=0).astype(jnp.bfloat16)
    cal_rows = gather_all_axes(calibration, TM, 0)
    running = jnp.dot(
        lax.all_gather(aligned, "col", axis=1, tiled=True),
        cal_rows,
        preferred_element_type=jnp.float32,
    )
    return running.astype(jnp.bfloat16)


def solution(mesh):
    torus = Mesh(mesh.devices.reshape(4, 4, mesh.shape["col"]), ("tm_0", "tm_1", "col"))
    in_specs = (
        P("col", TM, None),
        P("col", TM, None),
        P("col", TM),
        P("col", TM),
        P("col", TM, None),
        P("col", TM),
        P(TM, "col"),
    )
    out_specs = P(TM, "col")
    return jax.shard_map(
        per_device, mesh=torus, in_specs=in_specs, out_specs=out_specs, check_vma=False
    )
```

profile of v0, /device:TPU:1, one launch (start us, length us, event | category | flops | bytes accessed | tf_op | source)
XLA Modules:
  0.0 359.0 jit_solution(3384023761466500668)
XLA Ops:
  6.5 2.3 fusion.45
  8.8 0.0 all-gather.16.cloned.1.call-update
  8.8 0.0 all-gather.14.cloned.1.call-start
  8.9 0.7 all-gather.14.cloned.1.call-update
  9.6 0.0 all-gather.12.cloned.1.call-start
  9.6 33.4 %all-gather.16.cloned.1.call-done = bf16[2048,512]{1,0:T(8,128)(2,1)} async-done(((bf16[512,512]{1,0:T(8,128)(2,1)}), bf16[2048,512]{1,0:T(8,128)(2,1)}) %all-gather.16.cloned.1.call-update) | async-done | bytes 2097168 | tf_op jit(solution)/shard_map/all_gather | solution.py:20
  43.1 0.0 all-gather.12.cloned.1.call-update
  43.1 0.0 all-gather.10.cloned.1.call-start
  43.2 32.3 %all-gather.14.cloned.1.call-done = bf16[2048,512]{1,0:T(8,128)(2,1)} async-done(((bf16[512,512]{1,0:T(8,128)(2,1)}), bf16[2048,512]{1,0:T(8,128)(2,1)}) %all-gather.14.cloned.1.call-update) | async-done | bytes 2097168 | tf_op jit(solution)/shard_map/all_gather | solution.py:20
  75.4 0.0 all-gather.10.cloned.1.call-update
  75.4 1.5 fusion.38
  77.0 3.4 select_reduce_fusion
  80.4 0.0 copy-start
  80.4 17.4 %gather_fusion.1 = s32[3072]{0:T(1024)S(1)} fusion(s32[2048]{0:T(1024)S(1)} %bitcast.37, s32[3072]{0:T(1024)S(1)} %maximum_clamp_fusion), kind=kCustom, calls=%fused_computation.1 | custom fusion | bytes 36864 | tf_op jit(solution)/shard_map/jit(_take)/gather | solution.py:98
  97.9 0.7 select_n.64
  98.5 5.7 %all-to-all-start.1 = ((s32[16,1,192]{2,1,0:T(1,128)}), s32[16,1,192]{2,1,0:T(1,128)S(1)}, u32[]{:S(2)}, u32[]{:S(2)}) async-start(s32[16,1,192]{2,1,0:T(1,128)} %select_n.64), calls=%async_computation.1 | async-start | bytes 32768 | tf_op jit(solution)/shard_map/all_to_all | solution.py:104
  104.9 0.1 le.30
  104.9 0.1 ge.33
  105.0 8.1 %copy.20 = bf16[2048,1,128]{2,1,0:T(2,128)(2,1)S(1)} copy(bf16[2048,1,128]{2,0,1:T(8,128)(2,1)S(1)} %bitcast.46) | data formatting | bytes 1048576 | tf_op jit(solution)/shard_map/stack;squeeze | solution.py:93
  113.2 15.2 %broadcast_select_fusion.2 = bf16[2048,1,128]{2,1,0:T(2,128)(2,1)S(1)} fusion(pred[2048]{0:T(1024)(128)(4,1)S(1)} %iota_compare_fusion.37, bf16[2048,1,128]{2,0,1:T(8,128)(2,1)S(1)} %bitcast.47), kind=kLoop, calls=%fused_computation.42 | loop fusion | flops 262144 | bytes 1050624 | tf_op jit(solution)/shard_map/jit(_where)/select_n | solution.py:81
  128.4 2.4 pad_maximum_fusion.2
  130.8 10.4 %gather_fusion = bf16[3072,2,128]{2,1,0:T(2,128)(2,1)S(1)} fusion(bf16[2048,2,128]{2,1,0:T(2,128)(2,1)S(1)} %pad_maximum_fusion.2, s32[3072]{0:T(1024)S(1)} %maximum_clamp_fusion), kind=kCustom, calls=%fused_computation | custom fusion | bytes 3158016 | tf_op jit(solution)/shard_map/jit(_take)/gather | solution.py:95
  141.3 9.9 %broadcast_select_fusion.1 = bf16[16,192,2,128]{3,2,1,0:T(2,128)(2,1)} fusion(pred[16,192]{1,0:T(8,128)(4,1)S(1)} %ge.33, bf16[16,192,2,128]{3,2,1,0:T(2,128)(2,1)S(1)} %bitcast.43, pred[16,192]{1,0:T(8,128)(4,1)S(1)} %le.30), kind=kLoop, calls=%fused_computation.28 | loop fusion | flops 1572864 | bytes 3151872 | tf_op jit(solution)/shard_map/jit(_where)/select_n | solution.py:94
  151.2 6.7 %all-to-all-start = ((bf16[16,192,2,128]{3,2,1,0:T(2,128)(2,1)}), bf16[16,192,2,128]{3,2,1,0:T(2,128)(2,1)S(1)}, u32[]{:S(2)}, u32[]{:S(2)}) async-start(bf16[16,192,2,128]{3,2,1,0:T(2,128)(2,1)} %broadcast_select_fusion.1), calls=%async_computation | async-start | bytes 3145728 | tf_op jit(solution)/shard_map/all_to_all | solution.py:102
  158.0 0.0 all-gather.8.cloned.1.call-start
  158.1 0.1 eq.36
  158.2 20.8 %all-to-all-done = bf16[16,192,2,128]{3,2,1,0:T(2,128)(2,1)S(1)} async-done(((bf16[16,192,2,128]{3,2,1,0:T(2,128)(2,1)}), bf16[16,192,2,128]{3,2,1,0:T(2,128)(2,1)S(1)}, u32[]{:S(2)}, u32[]{:S(2)}) %all-to-all-start) | async-done | bytes 1572896 | tf_op jit(solution)/shard_map/all_to_all | solution.py:102
  178.9 2.6 fusion.44
  181.5 0.8 fusion.41
  182.4 0.8 slice_multiply_fusion.1
  183.1 0.6 pad_add_fusion
  183.8 0.2 fusion.37
  184.0 5.3 %fusion.6 = f32[128,2048]{1,0:T(8,128)S(1)} fusion(bf16[3072,128]{1,0:T(8,128)(2,1)S(1)} %get-tuple-element.8, s32[3072]{0:T(1024)S(1)} %eq.36), kind=kOutput, calls=%fused_computation.12 | convolution fusion | flops 1616904192 | bytes 1847296 | tf_op jit(solution)/shard_map/dot_general | solution.py:118
  189.3 5.3 %fusion = f32[128,2048]{1,0:T(8,128)S(1)} fusion(bf16[3072,128]{1,0:T(8,128)(2,1)S(1)} %get-tuple-element.8, s32[3072]{0:T(1024)S(1)} %get-tuple-element.20), kind=kOutput, calls=%fused_computation.3 | convolution fusion | flops 1616904192 | bytes 1847296 | tf_op jit(solution)/shard_map/dot_general | solution.py:118
  194.7 5.5 %fusion.2 = f32[128,2048]{1,0:T(8,128)S(1)} fusion(bf16[3072,128]{1,0:T(8,128)(2,1)S(1)} %get-tuple-element.8, s32[3072]{0:T(1024)S(1)} %get-tuple-element.21), kind=kOutput, calls=%fused_computation.6 | convolution fusion | flops 1616904192 | bytes 1847296 | tf_op jit(solution)/shard_map/dot_general | solution.py:118
  200.2 5.3 %fusion.4 = f32[128,2048]{1,0:T(8,128)S(1)} fusion(bf16[3072,128]{1,0:T(8,128)(2,1)S(1)} %get-tuple-element.8, s32[3072]{0:T(1024)S(1)} %get-tuple-element.19), kind=kOutput, calls=%fused_computation.9 | convolution fusion | flops 1616904192 | bytes 1847296 | tf_op jit(solution)/shard_map/dot_general | solution.py:118
  205.5 5.5 %fusion.21 = bf16[128,2048]{1,0:T(8,128)(2,1)S(1)} fusion(f32[128,2048]{1,0:T(8,128)S(1)} %fusion, bf16[3072,128]{1,0:T(8,128)(2,1)S(1)} %get-tuple-element.9, s32[3072]{0:T(1024)S(1)} %get-tuple-element.20), kind=kOutput, calls=%fused_computation.33 | convolution fusion | flops 1617428480 | bytes 2371584 | tf_op jit(solution)/shard_map/dot_general | solution.py:115
  211.1 5.3 %fusion.22 = bf16[128,2048]{1,0:T(8,128)(2,1)S(1)} fusion(f32[128,2048]{1,0:T(8,128)S(1)} %fusion.2, bf16[3072,128]{1,0:T(8,128)(2,1)S(1)} %get-tuple-element.9, s32[3072]{0:T(1024)S(1)} %get-tuple-element.21), kind=kOutput, calls=%fused_computation.34 | convolution fusion | flops 1617428480 | bytes 2371584 | tf_op jit(solution)/shard_map/dot_general | solution.py:115
  216.4 5.3 %fusion.23 = bf16[128,2048]{1,0:T(8,128)(2,1)S(1)} fusion(f32[128,2048]{1,0:T(8,128)S(1)} %fusion.4, bf16[3072,128]{1,0:T(8,128)(2,1)S(1)} %get-tuple-element.9, s32[3072]{0:T(1024)S(1)} %get-tuple-element.19), kind=kOutput, calls=%fused_computation.35 | convolution fusion | flops 1617428480 | bytes 2371584 | tf_op jit(solution)/shard_map/dot_general | solution.py:115
  221.8 5.6 %fusion.24 = bf16[128,2048]{1,0:T(8,128)(2,1)S(1)} fusion(f32[128,2048]{1,0:T(8,128)S(1)} %fusion.6, bf16[3072,128]{1,0:T(8,128)(2,1)S(1)} %get-tuple-element.9, s32[3072]{0:T(1024)S(1)} %eq.36), kind=kOutput, calls=%fused_computation.36 | convolution fusion | flops 1617428480 | bytes 2371584 | tf_op jit(solution)/shard_map/dot_general | solution.py:115
  227.4 1.4 pad_maximum_fusion.1
  228.8 0.0 all-gather.8.cloned.1.call-update
  228.8 0.0 all-gather.12.cloned.1.call-done
  228.9 7.3 %copy.22 = bf16[4,4,512,512]{3,2,0,1:T(8,128)(2,1)} copy(bf16[4,4,512,512]{3,2,1,0:T(8,128)(2,1)} %bitcast.42) | data formatting | bytes 16777216 | tf_op jit(solution)/shard_map/reshape | solution.py:22
  236.2 11.4 %all-gather.10.cloned.1.call-done = bf16[16,512,512]{2,1,0:T(8,128)(2,1)} async-done(((bf16[4,512,512]{2,1,0:T(8,128)(2,1)}), bf16[16,512,512]{2,1,0:T(8,128)(2,1)}) %all-gather.10.cloned.1.call-update) | async-done | bytes 8388624 | tf_op jit(solution)/shard_map/all_gather | solution.py:20
  247.6 13.9 %pad_maximum_fusion = bf16[16,1024,512]{2,1,0:T(8,128)(2,1)} fusion(bf16[16,512,512]{2,1,0:T(8,128)(2,1)} %bitcast.38, bf16[16,512,512]{2,1,0:T(8,128)(2,1)} %all-gather.10.cloned.1.call-done), kind=kLoop, calls=%fused_computation.16 | loop fusion | flops 33554432 | bytes 33554432 | tf_op jit(solution)/shard_map/concatenate | solution.py:42
  261.5 72.7 %all-gather.8.cloned.1.call-done = bf16[512,16384]{1,0:T(8,128)(2,1)} async-done(((bf16[512,2048]{1,0:T(8,128)(2,1)}), bf16[512,16384]{1,0:T(8,128)(2,1)}) %all-gather.8.cloned.1.call-update) | async-done | bytes 16777232 | tf_op jit(solution)/shard_map/all_gather | solution.py:125
  334.2 17.9 %convolution_convert_fusion = bf16[512,512]{1,0:T(8,128)(2,1)} fusion(bf16[512,16384]{1,0:T(8,128)(2,1)} %all-gather.8.cloned.1.call-done, bf16[16384,512]{1,0:T(8,128)(2,1)} %bitcast.41), kind=kOutput, calls=%fused_computation.61 | convolution fusion | flops 8590196736 | bytes 34078720 | tf_op jit(solution)/shard_map/dot_general | solution.py:124
  (18 shorter events, 0.1 us)
Async XLA Ops:
  6.5 68.9 %copy-start.2 = (s32[1,2048,1]{1,2,0:T(1,128)S(1)}, s32[1,2048,1]{1,2,0:T(1,128)}, u32[]{:S(2)}) copy-start(s32[1,2048,1]{1,2,0:T(1,128)} %param.11) | copy-start | bytes 24580
  6.5 36.5 %all-gather.16.cloned.1.call-start = ((), (), s32[]{:S(2)}) async-start(), calls=%async_computation.6 | async-start | bytes 2621440 | tf_op jit(solution)/shard_map/all_gather | solution.py:20
  8.8 66.6 %all-gather.14.cloned.1.call-start = ((), (), s32[]{:S(2)}) async-start(), calls=%async_computation.5 | async-start | bytes 2621440 | tf_op jit(solution)/shard_map/all_gather | solution.py:20
  9.6 219.3 %all-gather.12.cloned.1.call-start = ((), (), s32[]{:S(2)}) async-start(), calls=%async_computation.4 | async-start | bytes 10485760 | tf_op jit(solution)/shard_map/all_gather | solution.py:20
  43.1 37.3 %copy-start.3 = (s32[1,2048]{1,0:T(1,128)S(1)}, s32[1,2048]{1,0:T(1,128)}, u32[]{:S(2)}) copy-start(s32[1,2048]{1,0:T(1,128)} %param.9) | copy-start | bytes 24580
  43.1 37.3 %copy-start.4 = (s32[1,2048]{1,0:T(1,128)S(1)}, s32[1,2048]{1,0:T(1,128)}, u32[]{:S(2)}) copy-start(s32[1,2048]{1,0:T(1,128)} %param.10) | copy-start | bytes 24580
  43.1 204.5 %all-gather.10.cloned.1.call-start = ((), (), s32[]{:S(2)}) async-start(), calls=%async_computation.3 | async-start | bytes 10485760 | tf_op jit(solution)/shard_map/all_gather | solution.py:20
  80.4 24.6 %copy-start = (bf16[1,2048,128]{2,1,0:T(8,128)(2,1)S(1)}, bf16[1,2048,128]{2,1,0:T(8,128)(2,1)}, u32[]{:S(2)}) copy-start(bf16[1,2048,128]{2,1,0:T(8,128)(2,1)} %param.8) | copy-start | bytes 1572868
  80.4 32.8 %copy-start.1 = (bf16[1,2048,128]{2,1,0:T(8,128)(2,1)S(1)}, bf16[1,2048,128]{2,1,0:T(8,128)(2,1)}, u32[]{:S(2)}) copy-start(bf16[1,2048,128]{2,1,0:T(8,128)(2,1)} %param.7) | copy-start | bytes 1572868
  98.5 52.7 %all-to-all-start.1 = ((s32[16,1,192]{2,1,0:T(1,128)}), s32[16,1,192]{2,1,0:T(1,128)S(1)}, u32[]{:S(2)}, u32[]{:S(2)}) async-start(s32[16,1,192]{2,1,0:T(1,128)} %select_n.64), calls=%async_computation.1 | async-start | bytes 32768 | tf_op jit(solution)/shard_map/all_to_all | solution.py:104
  151.2 27.7 %all-to-all-start = ((bf16[16,192,2,128]{3,2,1,0:T(2,128)(2,1)}), bf16[16,192,2,128]{3,2,1,0:T(2,128)(2,1)S(1)}, u32[]{:S(2)}, u32[]{:S(2)}) async-start(bf16[16,192,2,128]{3,2,1,0:T(2,128)(2,1)} %broadcast_select_fusion.1), calls=%async_computation | async-start | bytes 3145728 | tf_op jit(solution)/shard_map/all_to_all | solution.py:102
  158.0 176.2 %all-gather.8.cloned.1.call-start = ((), (), s32[]{:S(2)}) async-start(), calls=%async_computation.2 | async-start | bytes 18874368 | tf_op jit(solution)/shard_map/all_gather | solution.py:125
Sparse Core Ops, SparseCore 0:
  9.0 34.0 all-gather.15
  44.7 30.6 all-gather.13
  77.1 83.2 all-gather.11
  161.9 85.6 all-gather.9
  249.1 84.9 all-gather.7
where the time goes:
time: 364 us; the launch traced here: 359 us
  waiting for transfers between devices  171 us (47%)
  matrix products  62.7 us (17%)
  other arithmetic  51.4 us (14%)
  local copies, waits for them, and re-layouts  46.6 us (13%)
  between operations  14.5 us (4%)
  starting transfers between devices  12.6 us (3%)
    all_gather x4, waiting for transfers between devices, gather_in_order(): parts = lax.all_gather(parts, axes[k], axis=0, tiled=True)  77.1 us
    all_gather x1, waiting for transfers between devices, per_device(): lax.all_gather(aligned, 'col', axis=1, tiled=True)  72.7 us
    dot_general x4, matrix products, per_device(): lax.dot_general(upper_part, place_onehot, dims, preferred_element_type=jn...  21.8 us
    dot_general x4, matrix products, per_device(): lax.dot_general(lower_part, place_onehot, dims, preferred_element_type=jn...  21.5 us
    all_to_all x1, waiting for transfers between devices, per_device(): lax.all_to_all(outgoing, TM, split_axis=0, concat_axis=0, tiled=True)  20.8 us
    dot_general x1, matrix products, per_device(): jnp.dot(lax.all_gather(aligned, 'col', axis=1, tiled=True), cal_rows, pre...  17.9 us
    gather x1, local copies, waits for them, and re-layouts, per_device(): jnp.take(row_keys, source_row, axis=0)  17.4 us
    select_n x1, other arithmetic, per_device(): values = jnp.where(is_live[:, None], values, jnp.zeros_like(values))  15.2 us
  transfers between devices with their start and end apart: 7, of which 5 were waited for; matrix products, arithmetic and copies ran while one was open for 39% of the time, Pallas kernels for 0%

commit v1 on v0

v1 whole, which is shorter than its diff:
```python
import jax
import jax.numpy as jnp
from jax import lax
from jax.experimental import pallas as pl
from jax.experimental.pallas import tpu as pltpu
from jax.sharding import Mesh
from jax.sharding import PartitionSpec as P

MESH = pl.DeviceIdType.MESH
F32 = jnp.float32
BF16 = jnp.bfloat16

LENGTH = 128
BLOCKS = 2048
OWNERS = 16
CAPACITY = 192
WINDOWS = 4
GROUP = 2048
ROWS = 512
COLS = 512
CAL_ROWS = 1024
HALF = CAL_ROWS // 2
MSG_ROWS = CAPACITY + 16
SLOTS = OWNERS * CAPACITY
CHUNK = 256
NT = (((1,), (1,)), ((), ()))


def kernel(
    values_ref,
    shifts_ref,
    sensor_ref,
    window_ref,
    owner_ref,
    cal_ref,
    out_ref,
    ranks,
    contrib,
    keys,
    outbuf,
    rx,
    placed,
    slot_sensor,
    aligned,
    calbuf,
    acc,
    give,
    take,
    a2a_s,
    a2a_r,
    x_s,
    x_r,
    cal_s,
    cal_r,
    d2d_s,
    d2d_r,
    ex_s,
    ex_r,
    own_sem,
):
    z, y, x, c = (lax.axis_index(name) for name in ("z", "y", "x", "c"))
    zp, zm, zo = (z + 1) % 4, (z + 3) % 4, (z + 2) % 4
    xp, xm, xo = (x + 1) % 4, (x + 3) % 4, (x + 2) % 4
    y2 = y % 2
    yq = y + 1 - 2 * y2
    sib = 1 - c
    me_t = z * 4 + y

    def piece(zz, row, half):
        return calbuf.at[c, zz * 2 + row, pl.ds(half * HALF, HALF), :]

    def own_piece(half):
        return cal_ref.at[pl.ds(half * HALF, HALF), :]

    def cal_copy(src, dst, sem, device):
        return pltpu.make_async_remote_copy(
            src_ref=src,
            dst_ref=dst,
            send_sem=cal_s.at[sem],
            recv_sem=cal_r.at[sem],
            device_id=device,
            device_id_type=MESH,
        )

    up, down, across = (zp, y, x, c), (zm, y, x, c), (z, yq, x, c)

    def send_up(k):
        src = (
            own_piece(0),
            own_piece(1),
            piece(zm, y2, 0),
            piece(z, 1 - y2, 0),
            piece(zm, 1 - y2, 0),
        )[k]
        dst = (
            piece(z, y2, 0),
            piece(z, y2, 1),
            piece(zm, y2, 0),
            piece(z, 1 - y2, 0),
            piece(zm, 1 - y2, 0),
        )[k]
        return cal_copy(src, dst, k, up)

    def send_down(k):
        src = (
            own_piece(1),
            own_piece(0),
            piece(zp, y2, 1),
            piece(z, 1 - y2, 1),
            piece(zp, 1 - y2, 1),
        )[k]
        dst = (
            piece(z, y2, 1),
            piece(z, y2, 0),
            piece(zp, y2, 1),
            piece(z, 1 - y2, 1),
            piece(zp, 1 - y2, 1),
        )[k]
        return cal_copy(src, dst, 5 + k, down)

    def send_across(k):
        src = (own_piece(0), own_piece(1), piece(zm, y2, 1), piece(zp, y2, 0))[k]
        dst = (piece(z, y2, 0), piece(z, y2, 1), piece(zm, y2, 1), piece(zp, y2, 0))[k]
        return cal_copy(src, dst, 10 + k, across)

    from_below = (
        (zm, y2, 0),
        (zm, y2, 1),
        (zo, y2, 0),
        (zm, 1 - y2, 0),
        (zo, 1 - y2, 0),
    )
    from_above = (
        (zp, y2, 1),
        (zp, y2, 0),
        (zo, y2, 1),
        (zp, 1 - y2, 1),
        (zo, 1 - y2, 1),
    )
    from_across = ((z, 1 - y2, 0), (z, 1 - y2, 1), (zm, 1 - y2, 1), (zp, 1 - y2, 0))

    def share(src, zz, row, half):
        at = (zz * 2 + row) * 2 + half
        return pltpu.make_async_remote_copy(
            src_ref=src,
            dst_ref=piece(zz, row, half),
            send_sem=d2d_s.at[at],
            recv_sem=d2d_r.at[at],
            device_id=(z, y, x, sib),
            device_id_type=MESH,
        )

    def arrive(sem, where, device):
        spot = piece(*where)
        cal_copy(spot, spot, sem, device).wait_recv()
        share(spot, *where).start()

    def arrive_below(k):
        arrive(k, from_below[k], down)

    def arrive_above(k):
        arrive(5 + k, from_above[k], up)

    def arrive_across(k):
        arrive(10 + k, from_across[k], across)

    own_copy = pltpu.make_async_copy(cal_ref, calbuf.at[c, z * 2 + y2], own_sem)

    send_up(0).start()
    send_down(0).start()
    send_across(0).start()
    own_copy.start()

    owner_row = owner_ref[...]
    mask = owner_row == lax.broadcasted_iota(jnp.int32, (OWNERS, BLOCKS), 0)
    maskf = mask.astype(F32)
    steps = BLOCKS // 128
    stack = jnp.concatenate(
        [maskf[:, j * 128 : (j + 1) * 128] for j in range(steps)], axis=0
    ).astype(BF16)
    row_id = lax.broadcasted_iota(jnp.int32, (128, 128), 0)
    col_id = lax.broadcasted_iota(jnp.int32, (128, 128), 1)
    strict = (row_id < col_id).astype(F32).astype(BF16)
    before = jnp.dot(stack, strict, preferred_element_type=F32)
    total = jnp.dot(stack, jnp.ones((128, 128), BF16), preferred_element_type=F32)
    offset = jnp.zeros((OWNERS, 128), F32)
    for j in range(steps):
        rank = before[j * OWNERS : (j + 1) * OWNERS] + offset
        ranks[:, j * 128 : (j + 1) * 128] = jnp.where(
            mask[:, j * 128 : (j + 1) * 128], rank.astype(jnp.int32), -1
        )
        offset = offset + total[j * OWNERS : (j + 1) * OWNERS]

    sensor = sensor_ref[...]
    kid = lax.broadcasted_iota(jnp.int32, (16, BLOCKS), 0)
    key_rows = jnp.where(
        kid == 0,
        sensor // 128,
        jnp.where(kid == 1, sensor % 128, jnp.where(kid == 2, window_ref[...], 0)),
    )
    keys[...] = key_rows.astype(F32).astype(BF16)

    lane = lax.broadcasted_iota(jnp.int32, (CHUNK, LENGTH), 1)

    @pl.loop(0, BLOCKS // CHUNK)
    def _(i):
        at = pl.ds(pl.multiple_of(i * CHUNK, CHUNK), CHUNK)
        samples = values_ref[at, :].astype(F32)
        offsets = shifts_ref[at, :].astype(F32)

        def product(k):
            weight = jnp.maximum(0.0, 1.0 - jnp.abs(offsets - k)).astype(BF16)
            return weight.astype(F32) * samples

        result = product(0.0)
        result = result + jnp.where(lane >= 1, pltpu.roll(product(1.0), 1, 1), 0.0)
        result = result + jnp.where(
            lane < LENGTH - 1, pltpu.roll(product(-1.0), LENGTH - 1, 1), 0.0
        )
        contrib[at, :] = result.astype(BF16)

    def destination(k):
        zd = (z + k // 4) % 4
        cd = k % 2
        yd = 2 * c + (k // 2) % 2
        yo = yd + cd * (3 - 2 * yd)
        return zd, yd, cd, zd * 4 + yo

    def message_copy(k, zd, yd, cd):
        return pltpu.make_async_remote_copy(
            src_ref=outbuf.at[k],
            dst_ref=rx.at[x, me_t],
            send_sem=a2a_s.at[k],
            recv_sem=a2a_r.at[me_t],
            device_id=(zd, yd, x, cd),
            device_id_type=MESH,
        )

    slot = lax.broadcasted_iota(jnp.int32, (256, BLOCKS), 0)
    slot = jnp.where(slot >= CAPACITY, slot - 64, slot)

    @pl.loop(0, OWNERS)
    def _(k):
        zd, yd, cd, owner = destination(k)
        pick = (ranks[pl.ds(owner, 1), :] == slot).astype(F32).astype(BF16)
        rows = jnp.dot(pick[:CAPACITY], contrib[...], preferred_element_type=F32)
        outbuf[k, 0:CAPACITY, :] = rows.astype(BF16)
        tags = lax.dot_general(keys[...], pick, NT, preferred_element_type=F32)
        tags = jnp.concatenate([tags[0:8, 0:128], tags[0:8, 128:256]], axis=0)
        outbuf[k, CAPACITY:MSG_ROWS, :] = tags.astype(BF16)
        is_self = (zd == z) & (yd == y) & (cd == c)

        @pl.when(jnp.logical_not(is_self))
        def _():
            message_copy(k, zd, yd, cd).start()

        @pl.when(is_self)
        def _():
            pltpu.make_async_copy(
                outbuf.at[k], rx.at[x, me_t], a2a_r.at[me_t]
            ).start()

    send_up(1).start()
    send_down(1).start()
    send_across(1).start()
    share(own_piece(0), z, y2, 0).start()
    share(own_piece(1), z, y2, 1).start()

    arrive_below(0)
    send_up(2).start()
    arrive_across(0)
    send_up(3).start()
    arrive_above(0)
    send_down(2).start()

    def x_copy(src_x, half, sem, device):
        span = rx.at[src_x, pl.ds(half * 8, 8)]
        return pltpu.make_async_remote_copy(
            src_ref=span,
            dst_ref=span,
            send_sem=x_s.at[sem],
            recv_sem=x_r.at[sem],
            device_id=device,
            device_id_type=MESH,
        )

    right, left = (z, y, xp, c), (z, y, xm, c)

    def message_wait(t):
        pltpu.make_async_copy(rx.at[x, t], rx.at[x, t], a2a_r.at[t]).wait()

    @pl.loop(0, 8)
    def _(t):
        message_wait(t)

    x_copy(x, 0, 0, right).start()

    @pl.loop(8, 16)
    def _(t):
        message_wait(t)

    x_copy(x, 1, 3, left).start()
    x_copy(x, 1, 1, right).start()
    x_copy(x, 0, 2, left).start()

    low_lanes = lax.broadcasted_iota(jnp.int32, (1, 128), 1) < 64

    def place(q):
        @pl.loop(0, OWNERS // 2)
        def _(p):
            m0 = rx.at[q, 2 * p]
            m1 = rx.at[q, 2 * p + 1]
            k0 = m0[CAPACITY:MSG_ROWS, :].astype(F32)
            k1 = m1[CAPACITY:MSG_ROWS, :].astype(F32)
            joint = jnp.where(low_lanes, k0[8:16], k1[8:16])
            tiles = (
                (m0[0:128, :], k0[0:8]),
                (m1[0:128, :], k1[0:8]),
                (
                    jnp.concatenate([m0[128:CAPACITY, :], m1[128:CAPACITY, :]], axis=0),
                    joint,
                ),
            )
            for n, (rows, tags) in enumerate(tiles):
                at = pl.ds(pl.multiple_of(p * 384 + n * 128, 128), 128)
                turned = rows.astype(F32).T
                slot_sensor[0:1, at] = (tags[0:1] * 128.0 + tags[1:2]).astype(jnp.int32)
                for w in range(WINDOWS):
                    placed[w * 128 : (w + 1) * 128, at] = jnp.where(
                        tags[2:3] == float(w), turned, 0.0
                    ).astype(BF16)

        @pl.loop(0, GROUP // CHUNK)
        def _(j):
            ids = lax.broadcasted_iota(jnp.int32, (CHUNK, SLOTS), 0) + j * CHUNK
            hot = (ids == slot_sensor[0:1, :]).astype(F32).astype(BF16)
            block = lax.dot_general(placed[...], hot, NT, preferred_element_type=F32)
            at = pl.ds(pl.multiple_of(j * CHUNK, CHUNK), CHUNK)
            aligned[q, :, at] = block.astype(BF16)

    place(x)

    arrive_below(1)
    arrive_above(1)
    send_across(2).start()
    send_across(3).start()
    arrive_across(1)
    send_down(3).start()

    x_copy(xm, 0, 0, left).wait_recv()
    x_copy(xm, 0, 4, right).start()
    x_copy(xp, 1, 3, right).wait_recv()
    x_copy(xp, 1, 5, left).start()
    x_copy(xm, 1, 1, left).wait_recv()
    place(xm)

    arrive_below(2)
    arrive_above(2)
    arrive_across(2)

    x_copy(xp, 0, 2, right).wait_recv()
    place(xp)

    arrive_below(3)
    send_up(4).start()
    arrive_above(3)
    send_down(4).start()
    arrive_across(3)

    x_copy(xo, 0, 4, left).wait_recv()
    x_copy(xo, 1, 5, right).wait_recv()
    place(xo)

    own_copy.wait()

    def shared(zz, row):
        for half in range(2):
            at = (zz * 2 + row) * 2 + half
            spot = calbuf.at[sib, zz * 2 + row, pl.ds(half * HALF, HALF), :]
            pltpu.make_async_remote_copy(
                src_ref=spot,
                dst_ref=spot,
                send_sem=d2d_s.at[at],
                recv_sem=d2d_r.at[at],
                device_id=(z, y, x, sib),
                device_id_type=MESH,
            ).wait_recv()

    acc[...] = jnp.zeros_like(acc)

    def multiply(zz):
        @pl.loop(0, 4)
        def _(it):
            row, panel = it // 2, it % 2
            at = pl.ds(pl.multiple_of(row * CAL_ROWS, CAL_ROWS), CAL_ROWS)
            acc[panel] += jnp.dot(
                aligned[zz, :, at], calbuf[panel, zz * 2 + row], preferred_element_type=F32
            )

    for zz in (z, zm, zp):
        shared(zz, 0)
        shared(zz, 1)
        multiply(zz)

    arrive_below(4)
    arrive_above(4)
    shared(zo, 0)
    shared(zo, 1)
    multiply(zo)

    give[...] = acc[...].astype(BF16)

    def exchange(panel, sem_s, sem_r, device):
        return pltpu.make_async_remote_copy(
            src_ref=give.at[panel],
            dst_ref=take.at[sem_r],
            send_sem=ex_s.at[sem_s],
            recv_sem=ex_r.at[sem_r],
            device_id=device,
            device_id_type=MESH,
        )

    @pl.when(c == 0)
    def _():
        over = exchange(1, 0, 0, (z, y, x, 1))
        over.start()
        exchange(0, 0, 0, (z, 3 - y, x, 1)).wait_recv()
        out_ref[...] = (acc[0] + take[0].astype(F32)).astype(BF16)
        over.wait_send()

    @pl.when(c == 1)
    def _():
        first = exchange(0, 0, 0, (z, 3 - y, x, 0))
        first.start()
        second = exchange(1, 1, 1, (z, 3 - y, x, 1))
        second.start()
        exchange(0, 0, 0, (z, y, x, 0)).wait_recv()
        exchange(1, 1, 1, (z, 3 - y, x, 1)).wait_recv()
        out_ref[...] = (take[0].astype(F32) + take[1].astype(F32)).astype(BF16)
        first.wait_send()
        second.wait_send()

    for k in range(5):
        send_up(k).wait_send()
        send_down(k).wait_send()
    for k in range(4):
        send_across(k).wait_send()
    share(own_piece(0), z, y2, 0).wait_send()
    share(own_piece(1), z, y2, 1).wait_send()
    for where in from_below + from_above + from_across:
        share(piece(*where), *where).wait_send()
    x_copy(x, 0, 0, right).wait_send()
    x_copy(x, 1, 1, right).wait_send()
    x_copy(x, 0, 2, left).wait_send()
    x_copy(x, 1, 3, left).wait_send()
    x_copy(xm, 0, 4, right).wait_send()
    x_copy(xp, 1, 5, left).wait_send()

    @pl.loop(0, OWNERS)
    def _(k):
        zd, yd, cd, _owner = destination(k)

        @pl.when(jnp.logical_not((zd == z) & (yd == y) & (cd == c)))
        def _():
            message_copy(k, zd, yd, cd).wait_send()


def per_device(
    block_values, block_shifts, block_sensor, block_window, block_owner, block_counts, calibration
):
    index = lax.broadcasted_iota(jnp.int32, (1, BLOCKS), 1)
    owner = jnp.where(index < block_counts[0, 0], block_owner.reshape(1, BLOCKS), -1)
    vmem = pl.BlockSpec(memory_space=pltpu.VMEM)
    return pl.pallas_call(
        kernel,
        out_shape=jax.ShapeDtypeStruct((ROWS, COLS), BF16),
        in_specs=[vmem] * 5 + [pl.BlockSpec(memory_space=pl.ANY)],
        out_specs=vmem,
        scratch_shapes=[
            pltpu.VMEM((OWNERS, BLOCKS), jnp.int32),
            pltpu.VMEM((BLOCKS, LENGTH), BF16),
            pltpu.VMEM((16, BLOCKS), BF16),
            pltpu.VMEM((OWNERS, MSG_ROWS, LENGTH), BF16),
            pltpu.VMEM((4, OWNERS, MSG_ROWS, LENGTH), BF16),
            pltpu.VMEM((ROWS, SLOTS), BF16),
            pltpu.VMEM((8, SLOTS), jnp.int32),
            pltpu.VMEM((4, ROWS, GROUP), BF16),
            pltpu.VMEM((2, 8, CAL_ROWS, COLS), BF16),
            pltpu.VMEM((2, ROWS, COLS), F32),
            pltpu.VMEM((2, ROWS, COLS), BF16),
            pltpu.VMEM((2, ROWS, COLS), BF16),
            pltpu.SemaphoreType.DMA((OWNERS,)),
            pltpu.SemaphoreType.DMA((OWNERS,)),
            pltpu.SemaphoreType.DMA((6,)),
            pltpu.SemaphoreType.DMA((6,)),
            pltpu.SemaphoreType.DMA((14,)),
            pltpu.SemaphoreType.DMA((14,)),
            pltpu.SemaphoreType.DMA((16,)),
            pltpu.SemaphoreType.DMA((16,)),
            pltpu.SemaphoreType.DMA((2,)),
            pltpu.SemaphoreType.DMA((2,)),
            pltpu.SemaphoreType.DMA,
        ],
        compiler_params=pltpu.CompilerParams(
            has_side_effects=True, vmem_limit_bytes=60 * 1024 * 1024
        ),
    )(
        block_values[0],
        block_shifts[0],
        block_sensor,
        block_window,
        owner,
        calibration,
    )


def solution(mesh):
    torus = Mesh(mesh.devices.reshape(4, 4, 4, 2), ("z", "y", "x", "c"))
    tm, col = ("z", "y"), ("x", "c")
    in_specs = (
        P(col, tm, None),
        P(col, tm, None),
        P(col, tm),
        P(col, tm),
        P(col, tm, None),
        P(col, tm),
        P(tm, col),
    )
    return jax.shard_map(
        per_device, mesh=torus, in_specs=in_specs, out_specs=P(tm, col), check_vma=False
    )
```

time: 364 us -> 122 us (0.34); the launches traced: 359 us -> 122 us
  waiting for transfers between devices: 171 us -> 0 us
  Pallas kernels: 0 us -> 118 us
  matrix products: 62.7 us -> 0 us
  other arithmetic: 51.4 us -> 1.31 us
  local copies, waits for them, and re-layouts: 46.6 us -> 1.87 us
  between operations: 14.5 us -> 0.66 us
  starting transfers between devices: 12.6 us -> 0 us
    all_gather x5 -> x0, waiting for transfers between devices: 150 us -> none  [the longest x4 77.1 us: gather_in_order(): parts = lax.all_gather(parts, axes[k], axis=0, tiled=True)]
    pallas_call x0 -> x1, Pallas kernels: none -> 118 us  [per_device(): pl.pallas_call(kernel, out_shape=jax.ShapeDtypeStruct((ROWS, COLS), BF16)...]
    dot_general x10 -> x0, matrix products: 62.7 us -> none  [the longest x4 21.8 us: per_device(): lax.dot_general(upper_part, place_onehot, dims, preferred_element_type=jn...]
    gather x2 -> x0, local copies, waits for them, and re-layouts: 27.8 us -> none  [the longest x1 17.4 us: per_device(): jnp.take(row_keys, source_row, axis=0)]
    select_n x3 -> x1, other arithmetic: 25.1 us -> 1.31 us  [per_device(): jnp.where(index < block_counts[0, 0], block_owner.reshape(1, BLOCKS), -1)]
    all_to_all x2 -> x0, waiting for transfers between devices: 20.8 us -> none  [the longest x1 20.8 us: per_device(): lax.all_to_all(outgoing, TM, split_axis=0, concat_axis=0, tiled=True)]
    concatenate x2 -> x0, other arithmetic: 15.3 us -> none  [the longest x1 13.9 us: gather_all_axes(): return joined_along(jnp.concatenate(outs, axis=cut + 1), dim)]
    all_to_all x2 -> x0, starting transfers between devices: 12.4 us -> none  [the longest x1 6.75 us: per_device(): lax.all_to_all(outgoing, TM, split_axis=0, concat_axis=0, tiled=True)]
  transfers between devices with their start and end apart: 7 -> 0, of which waited for: 5 -> 0; matrix products, arithmetic and copies ran while one was open for 39% -> 0% of each run, Pallas kernels for 0% -> 0%
where the time goes in v1:
time: 122 us
  Pallas kernels  118 us (97%)
  local copies, waits for them, and re-layouts  1.87 us (2%)
  other arithmetic  1.31 us (1%)
    pallas_call x1, Pallas kernels, per_device(): pl.pallas_call(kernel, out_shape=jax.ShapeDtypeStruct((ROWS, COLS), BF16)...  118 us

profile of v1, /device:TPU:1, one launch (start us, length us, event | category | flops | bytes accessed | tf_op | source)
XLA Modules:
  0.0 122.0 jit_solution(5400184559349831707)
XLA Ops:
  0.7 1.3 %compare_select_fusion.owner_ref = s32[1,2048]{1,0:T(1,128)} fusion(s32[1,2048,1]{1,2,0:T(1,128)} %param.11, s32[]{:T(128)} %bitcast.5), kind=kLoop, calls=%fused_computation | loop fusion | flops 4096 | bytes 16388 | tf_op jit(solution)/shard_map/jit(_where)/select_n | solution.py:472
  2.0 118.1 %shard_map.73 = bf16[512,512]{1,0:T(8,128)(2,1)} custom-call(bf16[2048,128]{1,0:T(8,128)(2,1)} %bitcast.6, bf16[2048,128]{1,0:T(8,128)(2,1)} %bitcast.7, s32[1,2048]{1,0:T(1,128)} %sensor_ref.1, s32[1,2048]{1,0:T(1,128)} %window_ref.1, s32[1,2048]{1,0:T(1,128)} %compare_select_fusion.owner_ref, bf16[1024,512]{1,0:T(8,128)(2,1)} %cal_ref.1), custom_call_target="tpu_custom_call" | custom-call | tf_op jit(solution)/shard_map/pallas_call | solution.py:474
  120.1 1.9 %copy.10 = bf16[512,512]{1,0:T(8,128)(2,1)} copy(bf16[512,512]{1,0:T(8,128)(2,1)} %shard_map.73) | data formatting | bytes 1048576

commit v2 on v1

--- a/solution.py
+++ b/solution.py
@@ -20,9 +20,11 @@
 COLS = 512
 CAL_ROWS = 1024
 HALF = CAL_ROWS // 2
-MSG_ROWS = CAPACITY + 16
+PAYLOAD = LENGTH + 16
+MSG_ROWS = PAYLOAD + PAYLOAD // 2
 SLOTS = OWNERS * CAPACITY
 CHUNK = 256
+WIDE = 1024
 NT = (((1,), (1,)), ((), ()))
 
 
@@ -32,15 +34,16 @@
     sensor_ref,
     window_ref,
     owner_ref,
+    count_ref,
     cal_ref,
     out_ref,
     ranks,
-    contrib,
-    keys,
+    payload,
     outbuf,
     rx,
     placed,
     slot_sensor,
+    hot,
     aligned,
     calbuf,
     acc,
@@ -166,12 +169,35 @@
 
     own_copy = pltpu.make_async_copy(cal_ref, calbuf.at[c, z * 2 + y2], own_sem)
 
+    barrier = pltpu.get_barrier_semaphore()
+
+    def greet(device):
+        pl.semaphore_signal(barrier, inc=1, device_id=device, device_id_type=MESH)
+
+    home = y // 2
+    for device in (up, down, across, (z, y, x, sib), (z, 3 - y, x, 1)):
+        greet(device)
+    for device in ((z, y, xp, c), (z, y, xm, c)):
+        greet(device)
+
+    @pl.loop(0, OWNERS)
+    def _(t):
+        zs, ys = t // 4, t % 4
+
+        @pl.when(jnp.logical_not((zs == z) & (ys == y) & (home == c)))
+        def _():
+            greet((zs, ys, x, home))
+
+    homed = home * c + (1 - home) * (1 - c)
+    pl.semaphore_wait(barrier, OWNERS + 6 + 2 * c - homed)
+
     send_up(0).start()
     send_down(0).start()
     send_across(0).start()
     own_copy.start()
 
-    owner_row = owner_ref[...]
+    live = lax.broadcasted_iota(jnp.int32, (1, BLOCKS), 1) < count_ref[...]
+    owner_row = jnp.where(live, owner_ref[...], -1)
     mask = owner_row == lax.broadcasted_iota(jnp.int32, (OWNERS, BLOCKS), 0)
     maskf = mask.astype(F32)
     steps = BLOCKS // 128
@@ -198,7 +224,7 @@
         sensor // 128,
         jnp.where(kid == 1, sensor % 128, jnp.where(kid == 2, window_ref[...], 0)),
     )
-    keys[...] = key_rows.astype(F32).astype(BF16)
+    payload[LENGTH:PAYLOAD, :] = key_rows.astype(F32).astype(BF16)
 
     lane = lax.broadcasted_iota(jnp.int32, (CHUNK, LENGTH), 1)
 
@@ -217,7 +243,7 @@
         result = result + jnp.where(
             lane < LENGTH - 1, pltpu.roll(product(-1.0), LENGTH - 1, 1), 0.0
         )
-        contrib[at, :] = result.astype(BF16)
+        payload[0:LENGTH, at] = result.T.astype(BF16)
 
     def destination(k):
         zd = (z + k // 4) % 4
@@ -236,18 +262,22 @@
             device_id_type=MESH,
         )
 
-    slot = lax.broadcasted_iota(jnp.int32, (256, BLOCKS), 0)
+    low_lanes = lax.broadcasted_iota(jnp.int32, (1, 128), 1) < 64
+    even = jnp.broadcast_to(y2, (1, 128)) == 0
+    slot = lax.broadcasted_iota(jnp.int16, (256, BLOCKS), 0)
     slot = jnp.where(slot >= CAPACITY, slot - 64, slot)
 
     @pl.loop(0, OWNERS)
     def _(k):
         zd, yd, cd, owner = destination(k)
-        pick = (ranks[pl.ds(owner, 1), :] == slot).astype(F32).astype(BF16)
-        rows = jnp.dot(pick[:CAPACITY], contrib[...], preferred_element_type=F32)
-        outbuf[k, 0:CAPACITY, :] = rows.astype(BF16)
-        tags = lax.dot_general(keys[...], pick, NT, preferred_element_type=F32)
-        tags = jnp.concatenate([tags[0:8, 0:128], tags[0:8, 128:256]], axis=0)
-        outbuf[k, CAPACITY:MSG_ROWS, :] = tags.astype(BF16)
+        rank = ranks[pl.ds(owner, 1), :].astype(jnp.int16)
+        pick = jnp.where(rank == slot, jnp.ones((), BF16), jnp.zeros((), BF16))
+        rows = lax.dot_general(payload[...], pick, NT, preferred_element_type=F32)
+        outbuf[k, 0:PAYLOAD, :] = rows[:, 0:128].astype(BF16)
+        top, bottom = rows[: PAYLOAD // 2, 128:256], rows[PAYLOAD // 2 :, 128:256]
+        outbuf[k, PAYLOAD:MSG_ROWS, :] = jnp.where(
+            low_lanes == even, top, bottom
+        ).astype(BF16)
         is_self = (zd == z) & (yd == y) & (cd == c)
 
         @pl.when(jnp.logical_not(is_self))
@@ -303,39 +333,39 @@
     x_copy(x, 1, 1, right).start()
     x_copy(x, 0, 2, left).start()
 
-    low_lanes = lax.broadcasted_iota(jnp.int32, (1, 128), 1) < 64
-
     def place(q):
         @pl.loop(0, OWNERS // 2)
         def _(p):
             m0 = rx.at[q, 2 * p]
             m1 = rx.at[q, 2 * p + 1]
-            k0 = m0[CAPACITY:MSG_ROWS, :].astype(F32)
-            k1 = m1[CAPACITY:MSG_ROWS, :].astype(F32)
-            joint = jnp.where(low_lanes, k0[8:16], k1[8:16])
+            r0 = m0[PAYLOAD:MSG_ROWS, :].astype(F32)
+            r1 = m1[PAYLOAD:MSG_ROWS, :].astype(F32)
+            upper = jnp.where(low_lanes, r0, r1)
+            lower = pltpu.roll(jnp.where(low_lanes, r1, r0), 64, 1)
+            joint = jnp.concatenate([upper, lower], axis=0)
             tiles = (
-                (m0[0:128, :], k0[0:8]),
-                (m1[0:128, :], k1[0:8]),
-                (
-                    jnp.concatenate([m0[128:CAPACITY, :], m1[128:CAPACITY, :]], axis=0),
-                    joint,
-                ),
+                m0[0:PAYLOAD, :].astype(F32),
+                m1[0:PAYLOAD, :].astype(F32),
+                joint,
             )
-            for n, (rows, tags) in enumerate(tiles):
+            for n, tile in enumerate(tiles):
                 at = pl.ds(pl.multiple_of(p * 384 + n * 128, 128), 128)
-                turned = rows.astype(F32).T
-                slot_sensor[0:1, at] = (tags[0:1] * 128.0 + tags[1:2]).astype(jnp.int32)
+                slot_sensor[0:1, at] = (
+                    tile[LENGTH : LENGTH + 1] * 128.0 + tile[LENGTH + 1 : LENGTH + 2]
+                ).astype(jnp.int32)
+                window = tile[LENGTH + 2 : LENGTH + 3]
                 for w in range(WINDOWS):
                     placed[w * 128 : (w + 1) * 128, at] = jnp.where(
-                        tags[2:3] == float(w), turned, 0.0
+                        window == float(w), tile[0:LENGTH], 0.0
                     ).astype(BF16)
 
-        @pl.loop(0, GROUP // CHUNK)
+        @pl.loop(0, GROUP // WIDE)
         def _(j):
-            ids = lax.broadcasted_iota(jnp.int32, (CHUNK, SLOTS), 0) + j * CHUNK
-            hot = (ids == slot_sensor[0:1, :]).astype(F32).astype(BF16)
-            block = lax.dot_general(placed[...], hot, NT, preferred_element_type=F32)
-            at = pl.ds(pl.multiple_of(j * CHUNK, CHUNK), CHUNK)
+            near = (slot_sensor[0:1, :] - j * WIDE).astype(jnp.int16)
+            ids = lax.broadcasted_iota(jnp.int16, (WIDE, SLOTS), 0)
+            hot[...] = jnp.where(ids == near, jnp.ones((), BF16), jnp.zeros((), BF16))
+            block = lax.dot_general(placed[...], hot[...], NT, preferred_element_type=F32)
+            at = pl.ds(pl.multiple_of(j * WIDE, WIDE), WIDE)
             aligned[q, :, at] = block.astype(BF16)
 
     place(x)
@@ -389,12 +419,11 @@
     acc[...] = jnp.zeros_like(acc)
 
     def multiply(zz):
-        @pl.loop(0, 4)
-        def _(it):
-            row, panel = it // 2, it % 2
-            at = pl.ds(pl.multiple_of(row * CAL_ROWS, CAL_ROWS), CAL_ROWS)
+        for panel in range(2):
             acc[panel] += jnp.dot(
-                aligned[zz, :, at], calbuf[panel, zz * 2 + row], preferred_element_type=F32
+                aligned[zz],
+                calbuf[panel, pl.ds(zz * 2, 2)].reshape(GROUP, COLS),
+                preferred_element_type=F32,
             )
 
     for zz in (z, zm, zp):
@@ -468,22 +497,20 @@
 def per_device(
     block_values, block_shifts, block_sensor, block_window, block_owner, block_counts, calibration
 ):
-    index = lax.broadcasted_iota(jnp.int32, (1, BLOCKS), 1)
-    owner = jnp.where(index < block_counts[0, 0], block_owner.reshape(1, BLOCKS), -1)
     vmem = pl.BlockSpec(memory_space=pltpu.VMEM)
     return pl.pallas_call(
         kernel,
         out_shape=jax.ShapeDtypeStruct((ROWS, COLS), BF16),
-        in_specs=[vmem] * 5 + [pl.BlockSpec(memory_space=pl.ANY)],
+        in_specs=[vmem] * 6 + [pl.BlockSpec(memory_space=pl.ANY)],
         out_specs=vmem,
         scratch_shapes=[
             pltpu.VMEM((OWNERS, BLOCKS), jnp.int32),
-            pltpu.VMEM((BLOCKS, LENGTH), BF16),
-            pltpu.VMEM((16, BLOCKS), BF16),
+            pltpu.VMEM((PAYLOAD, BLOCKS), BF16),
             pltpu.VMEM((OWNERS, MSG_ROWS, LENGTH), BF16),
             pltpu.VMEM((4, OWNERS, MSG_ROWS, LENGTH), BF16),
             pltpu.VMEM((ROWS, SLOTS), BF16),
             pltpu.VMEM((8, SLOTS), jnp.int32),
+            pltpu.VMEM((WIDE, SLOTS), BF16),
             pltpu.VMEM((4, ROWS, GROUP), BF16),
             pltpu.VMEM((2, 8, CAL_ROWS, COLS), BF16),
             pltpu.VMEM((2, ROWS, COLS), F32),
@@ -502,14 +529,15 @@
             pltpu.SemaphoreType.DMA,
         ],
         compiler_params=pltpu.CompilerParams(
-            has_side_effects=True, vmem_limit_bytes=60 * 1024 * 1024
+            collective_id=0, has_side_effects=True, vmem_limit_bytes=60 * 1024 * 1024
         ),
     )(
         block_values[0],
         block_shifts[0],
         block_sensor,
         block_window,
-        owner,
+        block_owner.reshape(1, BLOCKS),
+        block_counts,
         calibration,
     )
 

time: 122 us -> 109 us (0.89)
  Pallas kernels: 118 us -> 107 us
  other arithmetic: 1.31 us -> 0 us
    pallas_call x1, Pallas kernels: 118 us -> 107 us  [per_device(): pl.pallas_call(kernel, out_shape=jax.ShapeDtypeStruct((ROWS, COLS), BF16)...]
    select_n x1 -> x0, other arithmetic: 1.31 us -> none  [per_device(): jnp.where(index < block_counts[0, 0], block_owner.reshape(1, BLOCKS), -1)]
where the time goes in v2:
time: 109 us
  Pallas kernels  107 us (98%)
  local copies, waits for them, and re-layouts  1.87 us (2%)
    pallas_call x1, Pallas kernels, per_device(): pl.pallas_call(kernel, out_shape=jax.ShapeDtypeStruct((ROWS, COLS), BF16)...  107 us

profile of v2, /device:TPU:1, one launch (start us, length us, event | category | flops | bytes accessed | tf_op | source)
XLA Modules:
  0.0 109.1 jit_solution(223674654574600912)
XLA Ops:
  0.7 106.5 %shard_map.73 = bf16[512,512]{1,0:T(8,128)(2,1)} custom-call(bf16[2048,128]{1,0:T(8,128)(2,1)} %bitcast.3, bf16[2048,128]{1,0:T(8,128)(2,1)} %bitcast.4, s32[1,2048]{1,0:T(1,128)} %sensor_ref.1, s32[1,2048]{1,0:T(1,128)} %window_ref.1, s32[1,2048]{1,0:T(1,128)} %bitcast.5, s32[1,1]{1,0:T(1,128)S(6)} %copy.9.count_ref, bf16[1024,512]{1,0:T(8,128)(2,1)} %cal_ref.1), custom_call_target="tpu_custom_call" | custom-call | tf_op jit(solution)/shard_map/pallas_call | solution.py:501
  107.2 1.9 %copy.10 = bf16[512,512]{1,0:T(8,128)(2,1)} copy(bf16[512,512]{1,0:T(8,128)(2,1)} %shard_map.73) | data formatting | bytes 1048576

commit v3 on v2

v3 whole, which is shorter than its diff:
```python
import jax
import jax.numpy as jnp
from jax import lax
from jax.experimental import pallas as pl
from jax.experimental.pallas import tpu as pltpu
from jax.sharding import Mesh
from jax.sharding import PartitionSpec as P

MESH = pl.DeviceIdType.MESH
F32 = jnp.float32
BF16 = jnp.bfloat16

LENGTH = 128
BLOCKS = 2048
OWNERS = 16
CAPACITY = 192
WINDOWS = 4
GROUP = 2048
ROWS = 512
COLS = 512
CAL_ROWS = 1024
HALF = CAL_ROWS // 2
PARTS = 2
PART = COLS // PARTS
DEPTH = 4 * GROUP
PAYLOAD = LENGTH + 16
MSG_ROWS = PAYLOAD + PAYLOAD // 2
SLOTS = OWNERS * CAPACITY
CHUNK = 256
WIDE = 1024
NT = (((1,), (1,)), ((), ()))


def kernel(
    values_ref,
    shifts_ref,
    sensor_ref,
    window_ref,
    owner_ref,
    count_ref,
    cal_ref,
    out_ref,
    ranks,
    payload,
    outbuf,
    rx,
    placed,
    slot_sensor,
    hot,
    aligned,
    calbuf,
    acc,
    mine,
    give,
    take,
    a2a_s,
    a2a_r,
    x_s,
    x_r,
    cal_s,
    cal_r,
    d2d_s,
    d2d_r,
    ex_s,
    ex_r,
    own_sem,
):
    z, y, x, c = (lax.axis_index(name) for name in ("z", "y", "x", "c"))
    zp, zm, zo = (z + 1) % 4, (z + 3) % 4, (z + 2) % 4
    xp, xm, xo = (x + 1) % 4, (x + 3) % 4, (x + 2) % 4
    y2 = y % 2
    yq = y + 1 - 2 * y2
    sib = 1 - c
    me_t = z * 4 + y

    def lanes(core):
        return pl.ds(pl.multiple_of(core * PART, PART), PART)

    def piece(n, zz, row, half):
        at = pl.ds((zz * 2 + row) * CAL_ROWS + half * HALF, HALF)
        return calbuf.at[n, at, lanes(c)]

    def own_piece(n, half):
        return cal_ref.at[pl.ds(half * HALF, HALF), pl.ds(n * PART, PART)]

    def cal_copy(n, src, dst, sem, device):
        return pltpu.make_async_remote_copy(
            src_ref=src,
            dst_ref=dst,
            send_sem=cal_s.at[n * 14 + sem],
            recv_sem=cal_r.at[n * 14 + sem],
            device_id=device,
            device_id_type=MESH,
        )

    up, down, across = (zp, y, x, c), (zm, y, x, c), (z, yq, x, c)

    def relay(n, sem, spot, device):
        own = spot[0] is z and spot[1] is y2
        src = own_piece(n, spot[2]) if own else piece(n, *spot)
        return cal_copy(n, src, piece(n, *spot), sem, device)

    other = 1 - y2
    go_up = ((z, y2, 0), (z, y2, 1), (zm, y2, 0), (z, other, 0), (zm, other, 0))
    go_down = ((z, y2, 1), (z, y2, 0), (zp, y2, 1), (z, other, 1), (zp, other, 1))
    go_across = ((z, y2, 0), (z, y2, 1), (zm, y2, 1), (zp, y2, 0))

    def send_up(n, k):
        return relay(n, k, go_up[k], up)

    def send_down(n, k):
        return relay(n, 5 + k, go_down[k], down)

    def send_across(n, k):
        return relay(n, 10 + k, go_across[k], across)

    from_below = ((zm, y2, 0), (zm, y2, 1), (zo, y2, 0), (zm, other, 0), (zo, other, 0))
    from_above = ((zp, y2, 1), (zp, y2, 0), (zo, y2, 1), (zp, other, 1), (zo, other, 1))
    from_across = ((z, other, 0), (z, other, 1), (zm, other, 1), (zp, other, 0))

    def share(n, src, zz, row, half):
        at = n * 16 + (zz * 2 + row) * 2 + half
        return pltpu.make_async_remote_copy(
            src_ref=src,
            dst_ref=piece(n, zz, row, half),
            send_sem=d2d_s.at[at],
            recv_sem=d2d_r.at[at],
            device_id=(z, y, x, sib),
            device_id_type=MESH,
        )

    def arrive(n, sem, where, device):
        spot = piece(n, *where)
        cal_copy(n, spot, spot, sem, device).wait_recv()
        share(n, spot, *where).start()

    def below(n, k):
        arrive(n, k, from_below[k], down)

    def above(n, k):
        arrive(n, 5 + k, from_above[k], up)

    def beside(n, k):
        arrive(n, 10 + k, from_across[k], across)

    def own_copy(n):
        at = pl.ds((z * 2 + y2) * CAL_ROWS, CAL_ROWS)
        return pltpu.make_async_copy(
            cal_ref.at[:, pl.ds(n * PART, PART)], calbuf.at[n, at, lanes(c)], own_sem.at[n]
        )


    barrier = pltpu.get_barrier_semaphore()

    def greet(device):
        pl.semaphore_signal(barrier, inc=1, device_id=device, device_id_type=MESH)

    home = y // 2
    for device in (up, down, across, (z, y, x, sib), (z, 3 - y, x, 1)):
        greet(device)
    for device in ((z, y, xp, c), (z, y, xm, c)):
        greet(device)

    @pl.loop(0, OWNERS)
    def _(t):
        zs, ys = t // 4, t % 4

        @pl.when(jnp.logical_not((zs == z) & (ys == y) & (home == c)))
        def _():
            greet((zs, ys, x, home))

    homed = home * c + (1 - home) * (1 - c)
    pl.semaphore_wait(barrier, OWNERS + 6 + 2 * c - homed)

    def first(n):
        send_up(n, 0).start()
        send_down(n, 0).start()
        send_across(n, 0).start()

    def second(n):
        send_up(n, 1).start()
        send_down(n, 1).start()
        send_across(n, 1).start()

    def share_own(n):
        own_copy(n).start()
        for half in range(2):
            share(n, own_piece(n, half), z, y2, half).start()

    first(0)

    live = lax.broadcasted_iota(jnp.int32, (1, BLOCKS), 1) < count_ref[...]
    owner_row = jnp.where(live, owner_ref[...], -1)
    mask = owner_row == lax.broadcasted_iota(jnp.int32, (OWNERS, BLOCKS), 0)
    maskf = mask.astype(F32)
    steps = BLOCKS // 128
    stack = jnp.concatenate(
        [maskf[:, j * 128 : (j + 1) * 128] for j in range(steps)], axis=0
    ).astype(BF16)
    row_id = lax.broadcasted_iota(jnp.int32, (128, 128), 0)
    col_id = lax.broadcasted_iota(jnp.int32, (128, 128), 1)
    strict = (row_id < col_id).astype(F32).astype(BF16)
    before = jnp.dot(stack, strict, preferred_element_type=F32)
    total = jnp.dot(stack, jnp.ones((128, 128), BF16), preferred_element_type=F32)
    offset = jnp.zeros((OWNERS, 128), F32)
    for j in range(steps):
        rank = before[j * OWNERS : (j + 1) * OWNERS] + offset
        ranks[:, j * 128 : (j + 1) * 128] = jnp.where(
            mask[:, j * 128 : (j + 1) * 128], rank.astype(jnp.int32), -1
        )
        offset = offset + total[j * OWNERS : (j + 1) * OWNERS]

    sensor = sensor_ref[...]
    kid = lax.broadcasted_iota(jnp.int32, (16, BLOCKS), 0)
    key_rows = jnp.where(
        kid == 0,
        sensor // 128,
        jnp.where(kid == 1, sensor % 128, jnp.where(kid == 2, window_ref[...], 0)),
    )
    payload[LENGTH:PAYLOAD, :] = key_rows.astype(F32).astype(BF16)

    lane = lax.broadcasted_iota(jnp.int32, (CHUNK, LENGTH), 1)

    @pl.loop(0, BLOCKS // CHUNK)
    def _(i):
        at = pl.ds(pl.multiple_of(i * CHUNK, CHUNK), CHUNK)
        samples = values_ref[at, :].astype(F32)
        offsets = shifts_ref[at, :].astype(F32)

        def product(k):
            weight = jnp.maximum(0.0, 1.0 - jnp.abs(offsets - k)).astype(BF16)
            return weight.astype(F32) * samples

        result = product(0.0)
        result = result + jnp.where(lane >= 1, pltpu.roll(product(1.0), 1, 1), 0.0)
        result = result + jnp.where(
            lane < LENGTH - 1, pltpu.roll(product(-1.0), LENGTH - 1, 1), 0.0
        )
        payload[0:LENGTH, at] = result.T.astype(BF16)

    def destination(k):
        zd = (z + k // 4) % 4
        cd = k % 2
        yd = 2 * c + (k // 2) % 2
        yo = yd + cd * (3 - 2 * yd)
        return zd, yd, cd, zd * 4 + yo

    def message_copy(k, zd, yd, cd):
        return pltpu.make_async_remote_copy(
            src_ref=outbuf.at[k],
            dst_ref=rx.at[x, me_t],
            send_sem=a2a_s.at[k],
            recv_sem=a2a_r.at[me_t],
            device_id=(zd, yd, x, cd),
            device_id_type=MESH,
        )

    low_lanes = lax.broadcasted_iota(jnp.int32, (1, 128), 1) < 64
    even = jnp.broadcast_to(y2, (1, 128)) == 0
    lead_slot = lax.broadcasted_iota(jnp.int16, (128, BLOCKS), 0)
    tail_slot = lax.broadcasted_iota(jnp.int16, (64, BLOCKS), 0) + 128
    fold = PAYLOAD // 2

    def hit(owner, slot):
        rank = ranks[pl.ds(owner, 1), :].astype(jnp.int16)
        return jnp.where(rank == slot, jnp.ones((), BF16), jnp.zeros((), BF16))

    def send_message(k):
        zd, yd, cd, _owner = destination(k)
        is_self = (zd == z) & (yd == y) & (cd == c)

        @pl.when(jnp.logical_not(is_self))
        def _():
            message_copy(k, zd, yd, cd).start()

        @pl.when(is_self)
        def _():
            pltpu.make_async_copy(
                outbuf.at[k], rx.at[x, me_t], a2a_r.at[me_t]
            ).start()

    def messages(start, stop):
        @pl.loop(start, stop)
        def _(pair):
            k0, k1 = 2 * pair, 2 * pair + 1
            owner0, owner1 = destination(k0)[3], destination(k1)[3]
            pick = jnp.concatenate(
                [
                    hit(owner0, lead_slot),
                    hit(owner1, lead_slot),
                    hit(owner0, tail_slot),
                    hit(owner1, tail_slot),
                ],
                axis=0,
            )
            rows = lax.dot_general(payload[...], pick, NT, preferred_element_type=F32)
            outbuf[k0, 0:PAYLOAD, :] = rows[:, 0:128].astype(BF16)
            outbuf[k1, 0:PAYLOAD, :] = rows[:, 128:256].astype(BF16)
            tail = rows[:, 256:384]
            swapped = pltpu.roll(tail, 64, 1)
            near0 = jnp.where(even, tail[:fold], tail[fold:])
            far0 = jnp.where(even, swapped[fold:], swapped[:fold])
            near1 = jnp.where(even, swapped[:fold], swapped[fold:])
            far1 = jnp.where(even, tail[fold:], tail[:fold])
            outbuf[k0, PAYLOAD:MSG_ROWS, :] = jnp.where(low_lanes, near0, far0).astype(BF16)
            outbuf[k1, PAYLOAD:MSG_ROWS, :] = jnp.where(low_lanes, near1, far1).astype(BF16)
            send_message(k0)
            send_message(k1)

    def x_copy(src_x, group, sem, device):
        span = rx.at[src_x, pl.ds((z + 4 - group) % 4 * 4, 4)]
        return pltpu.make_async_remote_copy(
            src_ref=span,
            dst_ref=span,
            send_sem=x_s.at[sem],
            recv_sem=x_r.at[sem],
            device_id=device,
            device_id_type=MESH,
        )

    right, left = (z, y, xp, c), (z, y, xm, c)

    def spread(group):
        @pl.loop(0, 4)
        def _(i):
            t = (z + 4 - group) % 4 * 4 + i
            pltpu.make_async_copy(rx.at[x, t], rx.at[x, t], a2a_r.at[t]).wait()

        x_copy(x, group, group, right).start()
        x_copy(x, group, 4 + group, left).start()

    messages(0, 8)
    share_own(0)
    second(0)
    for group in range(4):
        spread(group)

    below(0, 0)
    beside(0, 0)
    above(0, 0)
    send_up(0, 2).start()
    send_down(0, 2).start()
    send_up(0, 3).start()
    first(1)
    share_own(1)
    acc[...] = jnp.zeros_like(acc)

    def prepare(q):
        @pl.loop(0, OWNERS // 2)
        def _(p):
            m0 = rx.at[q, 2 * p]
            m1 = rx.at[q, 2 * p + 1]
            r0 = m0[PAYLOAD:MSG_ROWS, :].astype(F32)
            r1 = m1[PAYLOAD:MSG_ROWS, :].astype(F32)
            upper = jnp.where(low_lanes, r0, r1)
            lower = pltpu.roll(jnp.where(low_lanes, r1, r0), 64, 1)
            joint = jnp.concatenate([upper, lower], axis=0)
            tiles = (
                m0[0:PAYLOAD, :].astype(F32),
                m1[0:PAYLOAD, :].astype(F32),
                joint,
            )
            for n, tile in enumerate(tiles):
                at = pl.ds(pl.multiple_of(p * 384 + n * 128, 128), 128)
                slot_sensor[0:1, at] = (
                    tile[LENGTH : LENGTH + 1] * 128.0 + tile[LENGTH + 1 : LENGTH + 2]
                ).astype(jnp.int32)
                window = tile[LENGTH + 2 : LENGTH + 3]
                for w in range(WINDOWS):
                    placed[w * 128 : (w + 1) * 128, at] = jnp.where(
                        window == float(w), tile[0:LENGTH], 0.0
                    ).astype(BF16)

    def place(q, j):
        near = (slot_sensor[0:1, :] - j * WIDE).astype(jnp.int16)
        ids = lax.broadcasted_iota(jnp.int16, (WIDE, SLOTS), 0)
        hot[...] = jnp.where(ids == near, jnp.ones((), BF16), jnp.zeros((), BF16))
        block = lax.dot_general(placed[...], hot[...], NT, preferred_element_type=F32)
        at = pl.ds(pl.multiple_of(q * GROUP + j * WIDE, WIDE), WIDE)
        aligned[:, at] = block.astype(BF16)

    def shared(n, zz):
        @pl.loop(0, 4)
        def _(i):
            at = n * 16 + zz * 4 + i
            spot = calbuf.at[n, pl.ds(zz * GROUP + i * HALF, HALF), lanes(sib)]
            pltpu.make_async_remote_copy(
                src_ref=spot,
                dst_ref=spot,
                send_sem=d2d_s.at[at],
                recv_sem=d2d_r.at[at],
                device_id=(z, y, x, sib),
                device_id_type=MESH,
            ).wait_recv()

    def multiply(n, zz):
        depth = pl.ds(pl.multiple_of(zz * GROUP, GROUP), GROUP)
        return jnp.dot(
            aligned[:, depth], calbuf[n, depth, :], preferred_element_type=F32
        )

    def early(n):
        own_copy(n).wait()
        for zz in (z, zm, zp):
            shared(n, zz)

        @pl.loop(0, 3)
        def _(i):
            acc[n] += multiply(n, (z + 3 * i - i // 2) % 4)

    def exchange(n, panel, sem_s, sem_r, device):
        return pltpu.make_async_remote_copy(
            src_ref=give.at[panel, n],
            dst_ref=take.at[sem_r, n],
            send_sem=ex_s.at[n * 2 + sem_s],
            recv_sem=ex_r.at[n * 2 + sem_r],
            device_id=device,
            device_id_type=MESH,
        )

    def late(n):
        shared(n, zo)
        total = acc[n] + multiply(n, zo)
        for panel in range(2):
            give[panel, n] = total[:, panel * PART : (panel + 1) * PART].astype(BF16)
        mine[n] = total[:, :PART]

        @pl.when(c == 0)
        def _():
            exchange(n, 1, 0, 0, (z, y, x, 1)).start()

        @pl.when(c == 1)
        def _():
            exchange(n, 0, 0, 0, (z, 3 - y, x, 0)).start()
            exchange(n, 1, 1, 1, (z, 3 - y, x, 1)).start()

    def finish(n):
        at = slice(n * PART, (n + 1) * PART)

        @pl.when(c == 0)
        def _():
            exchange(n, 0, 0, 0, (z, 3 - y, x, 1)).wait_recv()
            out_ref[:, at] = (mine[n] + take[0, n].astype(F32)).astype(BF16)
            exchange(n, 1, 0, 0, (z, y, x, 1)).wait_send()

        @pl.when(c == 1)
        def _():
            exchange(n, 0, 0, 0, (z, y, x, 0)).wait_recv()
            exchange(n, 1, 1, 1, (z, 3 - y, x, 1)).wait_recv()
            out_ref[:, at] = (take[0, n].astype(F32) + take[1, n].astype(F32)).astype(BF16)
            exchange(n, 0, 0, 0, (z, 3 - y, x, 0)).wait_send()
            exchange(n, 1, 1, 1, (z, 3 - y, x, 1)).wait_send()

    prepare(x)
    place(x, 0)
    beside(0, 1)
    send_down(0, 3).start()
    send_across(1, 1).start()
    place(x, 1)

    below(0, 1)
    above(0, 1)
    send_across(0, 2).start()
    send_across(0, 3).start()
    send_down(1, 1).start()
    send_up(1, 1).start()

    for group in range(2):
        x_copy(xm, group, group, left).wait_recv()
        x_copy(xm, group, 8 + group, right).start()
    for group in range(2, 4):
        x_copy(xp, group, 4 + group, right).wait_recv()
        x_copy(xp, group, 8 + group, left).start()
    x_copy(xm, 2, 2, left).wait_recv()
    x_copy(xm, 3, 3, left).wait_recv()

    prepare(xm)
    place(xm, 0)
    below(0, 3)
    send_up(0, 4).start()
    beside(1, 0)
    send_up(1, 3).start()
    beside(1, 1)
    send_down(1, 3).start()
    place(xm, 1)

    below(0, 2)
    above(0, 2)
    above(0, 3)
    send_down(0, 4).start()
    below(1, 0)
    send_up(1, 2).start()
    above(1, 0)
    send_down(1, 2).start()

    x_copy(xp, 0, 4, right).wait_recv()
    x_copy(xp, 1, 5, right).wait_recv()
    prepare(xp)
    place(xp, 0)
    below(1, 1)
    above(1, 1)
    send_across(1, 2).start()
    send_across(1, 3).start()
    beside(0, 2)
    beside(0, 3)
    place(xp, 1)

    x_copy(xo, 0, 8, left).wait_recv()
    x_copy(xo, 1, 9, left).wait_recv()
    x_copy(xo, 2, 10, right).wait_recv()
    x_copy(xo, 3, 11, right).wait_recv()
    prepare(xo)
    place(xo, 0)
    below(1, 3)
    send_up(1, 4).start()
    above(1, 3)
    send_down(1, 4).start()
    place(xo, 1)

    below(0, 4)
    above(0, 4)
    early(0)
    late(0)

    beside(1, 2)
    beside(1, 3)
    below(1, 2)
    above(1, 2)
    early(1)
    below(1, 4)
    above(1, 4)
    late(1)
    finish(0)
    finish(1)

    for n in range(PARTS):
        for k in range(5):
            send_up(n, k).wait_send()
            send_down(n, k).wait_send()
        for k in range(4):
            send_across(n, k).wait_send()

        @pl.loop(0, 16)
        def _(at):
            spot = calbuf.at[n, pl.ds(at * HALF, HALF), lanes(c)]
            pltpu.make_async_remote_copy(
                src_ref=spot,
                dst_ref=spot,
                send_sem=d2d_s.at[n * 16 + at],
                recv_sem=d2d_r.at[n * 16 + at],
                device_id=(z, y, x, sib),
                device_id_type=MESH,
            ).wait_send()

    for group in range(4):
        x_copy(x, group, group, right).wait_send()
        x_copy(x, group, 4 + group, left).wait_send()
    for group in range(2):
        x_copy(xm, group, 8 + group, right).wait_send()
        x_copy(xp, 2 + group, 10 + group, left).wait_send()

    @pl.loop(0, OWNERS)
    def _(k):
        zd, yd, cd, _owner = destination(k)

        @pl.when(jnp.logical_not((zd == z) & (yd == y) & (cd == c)))
        def _():
            message_copy(k, zd, yd, cd).wait_send()


def per_device(
    block_values, block_shifts, block_sensor, block_window, block_owner, block_counts, calibration
):
    vmem = pl.BlockSpec(memory_space=pltpu.VMEM)
    return pl.pallas_call(
        kernel,
        out_shape=jax.ShapeDtypeStruct((ROWS, COLS), BF16),
        in_specs=[vmem] * 6 + [pl.BlockSpec(memory_space=pl.ANY)],
        out_specs=vmem,
        scratch_shapes=[
            pltpu.VMEM((OWNERS, BLOCKS), jnp.int32),
            pltpu.VMEM((PAYLOAD, BLOCKS), BF16),
            pltpu.VMEM((OWNERS, MSG_ROWS, LENGTH), BF16),
            pltpu.VMEM((4, OWNERS, MSG_ROWS, LENGTH), BF16),
            pltpu.VMEM((ROWS, SLOTS), BF16),
            pltpu.VMEM((8, SLOTS), jnp.int32),
            pltpu.VMEM((WIDE, SLOTS), BF16),
            pltpu.VMEM((ROWS, DEPTH), BF16),
            pltpu.VMEM((PARTS, DEPTH, 2 * PART), BF16),
            pltpu.VMEM((PARTS, ROWS, 2 * PART), F32),
            pltpu.VMEM((PARTS, ROWS, PART), F32),
            pltpu.VMEM((2, PARTS, ROWS, PART), BF16),
            pltpu.VMEM((2, PARTS, ROWS, PART), BF16),
            pltpu.SemaphoreType.DMA((OWNERS,)),
            pltpu.SemaphoreType.DMA((OWNERS,)),
            pltpu.SemaphoreType.DMA((12,)),
            pltpu.SemaphoreType.DMA((12,)),
            pltpu.SemaphoreType.DMA((PARTS * 14,)),
            pltpu.SemaphoreType.DMA((PARTS * 14,)),
            pltpu.SemaphoreType.DMA((PARTS * 16,)),
            pltpu.SemaphoreType.DMA((PARTS * 16,)),
            pltpu.SemaphoreType.DMA((PARTS * 2,)),
            pltpu.SemaphoreType.DMA((PARTS * 2,)),
            pltpu.SemaphoreType.DMA((PARTS,)),
        ],
        compiler_params=pltpu.CompilerParams(
            collective_id=0, has_side_effects=True, vmem_limit_bytes=60 * 1024 * 1024
        ),
    )(
        block_values[0],
        block_shifts[0],
        block_sensor,
        block_window,
        block_owner.reshape(1, BLOCKS),
        block_counts,
        calibration,
    )


def solution(mesh):
    torus = Mesh(mesh.devices.reshape(4, 4, 4, 2), ("z", "y", "x", "c"))
    tm, col = ("z", "y"), ("x", "c")
    in_specs = (
        P(col, tm, None),
        P(col, tm, None),
        P(col, tm),
        P(col, tm),
        P(col, tm, None),
        P(col, tm),
        P(tm, col),
    )
    return jax.shard_map(
        per_device, mesh=torus, in_specs=in_specs, out_specs=P(tm, col), check_vma=False
    )
```

time: 109 us -> 96.6 us (0.89)
  Pallas kernels: 107 us -> 93.9 us
    pallas_call x1, Pallas kernels: 107 us -> 93.9 us  [per_device(): pl.pallas_call(kernel, out_shape=jax.ShapeDtypeStruct((ROWS, COLS), BF16)...]
where the time goes in v3:
time: 96.6 us; the launch traced here: 96.4 us
  Pallas kernels  93.9 us (97%)
  local copies, waits for them, and re-layouts  1.87 us (2%)
    pallas_call x1, Pallas kernels, per_device(): pl.pallas_call(kernel, out_shape=jax.ShapeDtypeStruct((ROWS, COLS), BF16)...  93.9 us

profile of v3, /device:TPU:1, one launch (start us, length us, event | category | flops | bytes accessed | tf_op | source)
XLA Modules:
  0.0 96.4 jit_solution(16620598636166280887)
XLA Ops:
  0.7 93.9 %shard_map.73 = bf16[512,512]{1,0:T(8,128)(2,1)} custom-call(bf16[2048,128]{1,0:T(8,128)(2,1)} %bitcast.3, bf16[2048,128]{1,0:T(8,128)(2,1)} %bitcast.4, s32[1,2048]{1,0:T(1,128)} %sensor_ref.1, s32[1,2048]{1,0:T(1,128)} %window_ref.1, s32[1,2048]{1,0:T(1,128)} %bitcast.5, s32[1,1]{1,0:T(1,128)S(6)} %copy.9.count_ref, bf16[1024,512]{1,0:T(8,128)(2,1)} %cal_ref.1), custom_call_target="tpu_custom_call" | custom-call | tf_op jit(solution)/shard_map/pallas_call | solution.py:575
  94.5 1.9 %copy.10 = bf16[512,512]{1,0:T(8,128)(2,1)} copy(bf16[512,512]{1,0:T(8,128)(2,1)} %shard_map.73) | data formatting | bytes 1048576

commit v4 on v3

--- a/solution.py
+++ b/solution.py
@@ -20,8 +20,11 @@
 COLS = 512
 CAL_ROWS = 1024
 HALF = CAL_ROWS // 2
-PARTS = 2
-PART = COLS // PARTS
+WIDTHS = (128, 128, 128, 128)
+PARTS = len(WIDTHS)
+STARTS = tuple(sum(WIDTHS[:n]) for n in range(PARTS))
+MOVES = 16
+EASED = (2,)
 DEPTH = 4 * GROUP
 PAYLOAD = LENGTH + 16
 MSG_ROWS = PAYLOAD + PAYLOAD // 2
@@ -53,6 +56,7 @@
     mine,
     give,
     take,
+    done,
     a2a_s,
     a2a_r,
     x_s,
@@ -64,6 +68,7 @@
     ex_s,
     ex_r,
     own_sem,
+    out_sem,
 ):
     z, y, x, c = (lax.axis_index(name) for name in ("z", "y", "x", "c"))
     zp, zm, zo = (z + 1) % 4, (z + 3) % 4, (z + 2) % 4
@@ -73,22 +78,26 @@
     sib = 1 - c
     me_t = z * 4 + y
 
-    def lanes(core):
-        return pl.ds(pl.multiple_of(core * PART, PART), PART)
+    def lanes(n, core):
+        at = 2 * STARTS[n] + core * WIDTHS[n]
+        return pl.ds(pl.multiple_of(at, 128), WIDTHS[n])
+
+    def both(n):
+        return slice(2 * STARTS[n], 2 * STARTS[n] + 2 * WIDTHS[n])
 
     def piece(n, zz, row, half):
         at = pl.ds((zz * 2 + row) * CAL_ROWS + half * HALF, HALF)
-        return calbuf.at[n, at, lanes(c)]
+        return calbuf.at[at, lanes(n, c)]
 
     def own_piece(n, half):
-        return cal_ref.at[pl.ds(half * HALF, HALF), pl.ds(n * PART, PART)]
+        return cal_ref.at[pl.ds(half * HALF, HALF), pl.ds(STARTS[n], WIDTHS[n])]
 
     def cal_copy(n, src, dst, sem, device):
         return pltpu.make_async_remote_copy(
             src_ref=src,
             dst_ref=dst,
-            send_sem=cal_s.at[n * 14 + sem],
-            recv_sem=cal_r.at[n * 14 + sem],
+            send_sem=cal_s.at[n],
+            recv_sem=cal_r.at[n * MOVES + sem],
             device_id=device,
             device_id_type=MESH,
         )
@@ -103,7 +112,14 @@
     other = 1 - y2
     go_up = ((z, y2, 0), (z, y2, 1), (zm, y2, 0), (z, other, 0), (zm, other, 0))
     go_down = ((z, y2, 1), (z, y2, 0), (zp, y2, 1), (z, other, 1), (zp, other, 1))
-    go_across = ((z, y2, 0), (z, y2, 1), (zm, y2, 1), (zp, y2, 0))
+    go_across = (
+        (z, y2, 0),
+        (z, y2, 1),
+        (zm, y2, 1),
+        (zp, y2, 0),
+        (zm, y2, 0),
+        (zp, y2, 1),
+    )
 
     def send_up(n, k):
         return relay(n, k, go_up[k], up)
@@ -116,15 +132,21 @@
 
     from_below = ((zm, y2, 0), (zm, y2, 1), (zo, y2, 0), (zm, other, 0), (zo, other, 0))
     from_above = ((zp, y2, 1), (zp, y2, 0), (zo, y2, 1), (zp, other, 1), (zo, other, 1))
-    from_across = ((z, other, 0), (z, other, 1), (zm, other, 1), (zp, other, 0))
+    from_across = (
+        (z, other, 0),
+        (z, other, 1),
+        (zm, other, 1),
+        (zp, other, 0),
+        (zm, other, 0),
+        (zp, other, 1),
+    )
 
     def share(n, src, zz, row, half):
-        at = n * 16 + (zz * 2 + row) * 2 + half
         return pltpu.make_async_remote_copy(
             src_ref=src,
             dst_ref=piece(n, zz, row, half),
-            send_sem=d2d_s.at[at],
-            recv_sem=d2d_r.at[at],
+            send_sem=d2d_s.at[n],
+            recv_sem=d2d_r.at[2 * n + (1 if zz is zo else 0)],
             device_id=(z, y, x, sib),
             device_id_type=MESH,
         )
@@ -146,9 +168,10 @@
     def own_copy(n):
         at = pl.ds((z * 2 + y2) * CAL_ROWS, CAL_ROWS)
         return pltpu.make_async_copy(
-            cal_ref.at[:, pl.ds(n * PART, PART)], calbuf.at[n, at, lanes(c)], own_sem.at[n]
-        )
-
+            cal_ref.at[:, pl.ds(STARTS[n], WIDTHS[n])],
+            calbuf.at[at, lanes(n, c)],
+            own_sem.at[n],
+        )
 
     barrier = pltpu.get_barrier_semaphore()
 
@@ -169,8 +192,6 @@
         def _():
             greet((zs, ys, x, home))
 
-    homed = home * c + (1 - home) * (1 - c)
-    pl.semaphore_wait(barrier, OWNERS + 6 + 2 * c - homed)
 
     def first(n):
         send_up(n, 0).start()
@@ -186,8 +207,6 @@
         own_copy(n).start()
         for half in range(2):
             share(n, own_piece(n, half), z, y2, half).start()
-
-    first(0)
 
     live = lax.broadcasted_iota(jnp.int32, (1, BLOCKS), 1) < count_ref[...]
     owner_row = jnp.where(live, owner_ref[...], -1)
@@ -249,8 +268,8 @@
         return pltpu.make_async_remote_copy(
             src_ref=outbuf.at[k],
             dst_ref=rx.at[x, me_t],
-            send_sem=a2a_s.at[k],
-            recv_sem=a2a_r.at[me_t],
+            send_sem=a2a_s,
+            recv_sem=a2a_r.at[k // 4],
             device_id=(zd, yd, x, cd),
             device_id_type=MESH,
         )
@@ -276,7 +295,7 @@
         @pl.when(is_self)
         def _():
             pltpu.make_async_copy(
-                outbuf.at[k], rx.at[x, me_t], a2a_r.at[me_t]
+                outbuf.at[k], rx.at[x, me_t], a2a_r.at[k // 4]
             ).start()
 
     def messages(start, stop):
@@ -312,7 +331,7 @@
         return pltpu.make_async_remote_copy(
             src_ref=span,
             dst_ref=span,
-            send_sem=x_s.at[sem],
+            send_sem=x_s,
             recv_sem=x_r.at[sem],
             device_id=device,
             device_id_type=MESH,
@@ -321,28 +340,14 @@
     right, left = (z, y, xp, c), (z, y, xm, c)
 
     def spread(group):
-        @pl.loop(0, 4)
-        def _(i):
-            t = (z + 4 - group) % 4 * 4 + i
-            pltpu.make_async_copy(rx.at[x, t], rx.at[x, t], a2a_r.at[t]).wait()
+        span = rx.at[x, pl.ds((z + 4 - group) % 4 * 4, 4)]
+        pltpu.make_async_copy(span, span, a2a_r.at[group]).wait()
 
         x_copy(x, group, group, right).start()
         x_copy(x, group, 4 + group, left).start()
 
-    messages(0, 8)
-    share_own(0)
-    second(0)
-    for group in range(4):
-        spread(group)
-
-    below(0, 0)
-    beside(0, 0)
-    above(0, 0)
-    send_up(0, 2).start()
-    send_down(0, 2).start()
-    send_up(0, 3).start()
-    first(1)
-    share_own(1)
+    homed = home * c + (1 - home) * (1 - c)
+    pl.semaphore_wait(barrier, OWNERS + 6 + 2 * c - homed)
     acc[...] = jnp.zeros_like(acc)
 
     def prepare(q):
@@ -379,39 +384,30 @@
         at = pl.ds(pl.multiple_of(q * GROUP + j * WIDE, WIDE), WIDE)
         aligned[:, at] = block.astype(BF16)
 
-    def shared(n, zz):
-        @pl.loop(0, 4)
-        def _(i):
-            at = n * 16 + zz * 4 + i
-            spot = calbuf.at[n, pl.ds(zz * GROUP + i * HALF, HALF), lanes(sib)]
-            pltpu.make_async_remote_copy(
-                src_ref=spot,
-                dst_ref=spot,
-                send_sem=d2d_s.at[at],
-                recv_sem=d2d_r.at[at],
-                device_id=(z, y, x, sib),
-                device_id_type=MESH,
-            ).wait_recv()
+    def shared(n, final):
+        rows = 4 if final else 12
+        spot = calbuf.at[pl.ds(0, rows * HALF), lanes(n, sib)]
+        pltpu.make_async_copy(spot, spot, d2d_r.at[2 * n + final]).wait()
 
     def multiply(n, zz):
         depth = pl.ds(pl.multiple_of(zz * GROUP, GROUP), GROUP)
         return jnp.dot(
-            aligned[:, depth], calbuf[n, depth, :], preferred_element_type=F32
+            aligned[:, depth], calbuf[depth, both(n)], preferred_element_type=F32
         )
 
     def early(n):
         own_copy(n).wait()
-        for zz in (z, zm, zp):
-            shared(n, zz)
+        shared(n, 0)
 
         @pl.loop(0, 3)
         def _(i):
-            acc[n] += multiply(n, (z + 3 * i - i // 2) % 4)
+            acc[:, both(n)] += multiply(n, (z + 3 * i - i // 2) % 4)
 
     def exchange(n, panel, sem_s, sem_r, device):
+        at = pl.ds(STARTS[n], WIDTHS[n])
         return pltpu.make_async_remote_copy(
-            src_ref=give.at[panel, n],
-            dst_ref=take.at[sem_r, n],
+            src_ref=give.at[panel, :, at],
+            dst_ref=take.at[sem_r, :, at],
             send_sem=ex_s.at[n * 2 + sem_s],
             recv_sem=ex_r.at[n * 2 + sem_r],
             device_id=device,
@@ -419,11 +415,13 @@
         )
 
     def late(n):
-        shared(n, zo)
-        total = acc[n] + multiply(n, zo)
+        shared(n, 1)
+        total = acc[:, both(n)] + multiply(n, zo)
+        width = WIDTHS[n]
+        at = slice(STARTS[n], STARTS[n] + width)
         for panel in range(2):
-            give[panel, n] = total[:, panel * PART : (panel + 1) * PART].astype(BF16)
-        mine[n] = total[:, :PART]
+            give[panel, :, at] = total[:, panel * width : (panel + 1) * width].astype(BF16)
+        mine[:, at] = total[:, :width]
 
         @pl.when(c == 0)
         def _():
@@ -434,138 +432,211 @@
             exchange(n, 0, 0, 0, (z, 3 - y, x, 0)).start()
             exchange(n, 1, 1, 1, (z, 3 - y, x, 1)).start()
 
+    def out_copy(n):
+        return pltpu.make_async_copy(
+            done.at[:, pl.ds(STARTS[n], WIDTHS[n])],
+            out_ref.at[:, pl.ds(STARTS[n], WIDTHS[n])],
+            out_sem.at[n],
+        )
+
     def finish(n):
-        at = slice(n * PART, (n + 1) * PART)
+        at = slice(STARTS[n], STARTS[n] + WIDTHS[n])
 
         @pl.when(c == 0)
         def _():
             exchange(n, 0, 0, 0, (z, 3 - y, x, 1)).wait_recv()
-            out_ref[:, at] = (mine[n] + take[0, n].astype(F32)).astype(BF16)
+            done[:, at] = (mine[:, at] + take[0, :, at].astype(F32)).astype(BF16)
+            out_copy(n).start()
             exchange(n, 1, 0, 0, (z, y, x, 1)).wait_send()
 
         @pl.when(c == 1)
         def _():
             exchange(n, 0, 0, 0, (z, y, x, 0)).wait_recv()
             exchange(n, 1, 1, 1, (z, 3 - y, x, 1)).wait_recv()
-            out_ref[:, at] = (take[0, n].astype(F32) + take[1, n].astype(F32)).astype(BF16)
+            done[:, at] = (take[0, :, at].astype(F32) + take[1, :, at].astype(F32)).astype(BF16)
+            out_copy(n).start()
             exchange(n, 0, 0, 0, (z, 3 - y, x, 0)).wait_send()
             exchange(n, 1, 1, 1, (z, 3 - y, x, 1)).wait_send()
 
+    messages(0, 8)
+    send_up(0, 0).start()
+    send_down(0, 0).start()
+    send_across(0, 0).start()
+    share_own(0)
+    spread(0)
+    spread(1)
+    send_up(0, 1).start()
+    send_up(1, 0).start()
+    share_own(1)
+    send_down(0, 1).start()
+    send_down(1, 0).start()
+    send_across(0, 1).start()
+    send_across(1, 0).start()
+    spread(2)
+    spread(3)
     prepare(x)
+    send_up(1, 1).start()
+    send_down(1, 1).start()
+    send_across(1, 1).start()
     place(x, 0)
+    above(0, 0)
+    send_down(0, 2).start()
+    below(0, 0)
+    send_up(0, 2).start()
+    beside(0, 0)
+    send_up(0, 3).start()
+    send_down(2, 0).start()
+    share_own(2)
+    send_across(2, 0).start()
+    send_across(2, 1).start()
+    place(x, 1)
     beside(0, 1)
     send_down(0, 3).start()
-    send_across(1, 1).start()
-    place(x, 1)
-
+    above(0, 1)
+    send_across(0, 3).start()
     below(0, 1)
-    above(0, 1)
     send_across(0, 2).start()
-    send_across(0, 3).start()
-    send_down(1, 1).start()
-    send_up(1, 1).start()
-
-    for group in range(2):
-        x_copy(xm, group, group, left).wait_recv()
-        x_copy(xm, group, 8 + group, right).start()
-    for group in range(2, 4):
-        x_copy(xp, group, 4 + group, right).wait_recv()
-        x_copy(xp, group, 8 + group, left).start()
+    above(1, 0)
+    send_down(1, 2).start()
+    beside(1, 0)
+    send_up(1, 3).start()
+    below(1, 0)
+    send_up(1, 2).start()
+    x_copy(xm, 0, 0, left).wait_recv()
+    x_copy(xm, 0, 8, right).start()
+    x_copy(xm, 1, 1, left).wait_recv()
+    x_copy(xm, 1, 9, right).start()
+    x_copy(xp, 2, 6, right).wait_recv()
+    x_copy(xp, 2, 10, left).start()
+    x_copy(xp, 3, 7, right).wait_recv()
+    x_copy(xp, 3, 11, left).start()
+    below(1, 1)
+    send_across(1, 2).start()
+    above(1, 1)
+    send_across(1, 3).start()
+    beside(1, 1)
+    send_down(1, 3).start()
+    send_up(2, 0).start()
     x_copy(xm, 2, 2, left).wait_recv()
     x_copy(xm, 3, 3, left).wait_recv()
-
     prepare(xm)
     place(xm, 0)
     below(0, 3)
     send_up(0, 4).start()
-    beside(1, 0)
-    send_up(1, 3).start()
-    beside(1, 1)
-    send_down(1, 3).start()
-    place(xm, 1)
-
     below(0, 2)
     above(0, 2)
+    above(2, 0)
+    send_down(2, 2).start()
+    send_across(2, 5).start()
+    beside(2, 0)
+    beside(2, 1)
+    send_up(2, 1).start()
+    send_up(3, 0).start()
+    share_own(3)
+    send_down(2, 1).start()
+    send_down(3, 0).start()
+    place(xm, 1)
+    below(1, 3)
+    send_up(1, 4).start()
+    below(1, 2)
     above(0, 3)
     send_down(0, 4).start()
-    below(1, 0)
-    send_up(1, 2).start()
-    above(1, 0)
-    send_down(1, 2).start()
-
+    above(1, 2)
+    above(1, 3)
+    send_down(1, 4).start()
+    below(2, 0)
+    send_up(2, 2).start()
+    send_across(2, 4).start()
+    beside(0, 3)
+    beside(0, 2)
     x_copy(xp, 0, 4, right).wait_recv()
     x_copy(xp, 1, 5, right).wait_recv()
     prepare(xp)
+    send_across(3, 0).start()
     place(xp, 0)
-    below(1, 1)
-    above(1, 1)
-    send_across(1, 2).start()
-    send_across(1, 3).start()
-    beside(0, 2)
-    beside(0, 3)
+    beside(1, 2)
+    beside(1, 3)
     place(xp, 1)
-
+    beside(2, 5)
+    send_down(2, 4).start()
+    send_across(3, 1).start()
     x_copy(xo, 0, 8, left).wait_recv()
     x_copy(xo, 1, 9, left).wait_recv()
     x_copy(xo, 2, 10, right).wait_recv()
     x_copy(xo, 3, 11, right).wait_recv()
     prepare(xo)
+    send_up(3, 1).start()
     place(xo, 0)
-    below(1, 3)
-    send_up(1, 4).start()
-    above(1, 3)
-    send_down(1, 4).start()
+    beside(2, 4)
+    send_up(2, 4).start()
+    beside(3, 0)
+    send_up(3, 3).start()
+    below(2, 1)
+    send_across(2, 2).start()
+    below(3, 0)
+    send_up(3, 2).start()
+    below(0, 4)
+    above(3, 0)
+    send_down(3, 2).start()
+    above(2, 1)
+    send_across(2, 3).start()
+    above(2, 2)
+    send_down(3, 1).start()
     place(xo, 1)
-
-    below(0, 4)
+    beside(3, 1)
+    send_down(3, 3).start()
+    below(1, 4)
+    below(2, 2)
     above(0, 4)
+    above(1, 4)
     early(0)
     late(0)
-
-    beside(1, 2)
-    beside(1, 3)
-    below(1, 2)
-    above(1, 2)
+    above(2, 4)
     early(1)
-    below(1, 4)
-    above(1, 4)
+    below(3, 1)
+    send_across(3, 2).start()
     late(1)
+    beside(2, 3)
+    beside(2, 2)
+    early(2)
+    above(3, 1)
+    send_across(3, 3).start()
+    above(3, 2)
+    above(3, 3)
+    send_down(3, 4).start()
+    below(3, 2)
+    below(3, 3)
+    send_up(3, 4).start()
+    below(2, 4)
+    late(2)
+    beside(3, 2)
+    beside(3, 3)
+    below(3, 4)
+    above(3, 4)
+    early(3)
+    late(3)
+    def sent(ref, sem):
+        pltpu.make_async_copy(ref, ref, sem).wait()
+
+    for n in range(PARTS):
+        sent(calbuf.at[pl.ds(0, 14 * HALF), lanes(n, c)], cal_s.at[n])
+        sent(calbuf.at[:, lanes(n, c)], d2d_s.at[n])
+    sent(rx.at[pl.ds(0, 3)], x_s)
+
+    @pl.when(home == c)
+    def _():
+        sent(outbuf.at[pl.ds(0, OWNERS - 1)], a2a_s)
+
+    @pl.when(home != c)
+    def _():
+        sent(outbuf, a2a_s)
+
     finish(0)
     finish(1)
-
+    finish(2)
+    finish(3)
     for n in range(PARTS):
-        for k in range(5):
-            send_up(n, k).wait_send()
-            send_down(n, k).wait_send()
-        for k in range(4):
-            send_across(n, k).wait_send()
-
-        @pl.loop(0, 16)
-        def _(at):
-            spot = calbuf.at[n, pl.ds(at * HALF, HALF), lanes(c)]
-            pltpu.make_async_remote_copy(
-                src_ref=spot,
-                dst_ref=spot,
-                send_sem=d2d_s.at[n * 16 + at],
-                recv_sem=d2d_r.at[n * 16 + at],
-                device_id=(z, y, x, sib),
-                device_id_type=MESH,
-            ).wait_send()
-
-    for group in range(4):
-        x_copy(x, group, group, right).wait_send()
-        x_copy(x, group, 4 + group, left).wait_send()
-    for group in range(2):
-        x_copy(xm, group, 8 + group, right).wait_send()
-        x_copy(xp, 2 + group, 10 + group, left).wait_send()
-
-    @pl.loop(0, OWNERS)
-    def _(k):
-        zd, yd, cd, _owner = destination(k)
-
-        @pl.when(jnp.logical_not((zd == z) & (yd == y) & (cd == c)))
-        def _():
-            message_copy(k, zd, yd, cd).wait_send()
+        out_copy(n).wait()
 
 
 def per_device(
@@ -576,7 +647,7 @@
         kernel,
         out_shape=jax.ShapeDtypeStruct((ROWS, COLS), BF16),
         in_specs=[vmem] * 6 + [pl.BlockSpec(memory_space=pl.ANY)],
-        out_specs=vmem,
+        out_specs=pl.BlockSpec(memory_space=pl.ANY),
         scratch_shapes=[
             pltpu.VMEM((OWNERS, BLOCKS), jnp.int32),
             pltpu.VMEM((PAYLOAD, BLOCKS), BF16),
@@ -586,21 +657,23 @@
             pltpu.VMEM((8, SLOTS), jnp.int32),
             pltpu.VMEM((WIDE, SLOTS), BF16),
             pltpu.VMEM((ROWS, DEPTH), BF16),
-            pltpu.VMEM((PARTS, DEPTH, 2 * PART), BF16),
-            pltpu.VMEM((PARTS, ROWS, 2 * PART), F32),
-            pltpu.VMEM((PARTS, ROWS, PART), F32),
-            pltpu.VMEM((2, PARTS, ROWS, PART), BF16),
-            pltpu.VMEM((2, PARTS, ROWS, PART), BF16),
-            pltpu.SemaphoreType.DMA((OWNERS,)),
-            pltpu.SemaphoreType.DMA((OWNERS,)),
+            pltpu.VMEM((DEPTH, 2 * COLS), BF16),
+            pltpu.VMEM((ROWS, 2 * COLS), F32),
+            pltpu.VMEM((ROWS, COLS), F32),
+            pltpu.VMEM((2, ROWS, COLS), BF16),
+            pltpu.VMEM((2, ROWS, COLS), BF16),
+            pltpu.VMEM((ROWS, COLS), BF16),
+            pltpu.SemaphoreType.DMA,
+            pltpu.SemaphoreType.DMA((4,)),
+            pltpu.SemaphoreType.DMA,
             pltpu.SemaphoreType.DMA((12,)),
-            pltpu.SemaphoreType.DMA((12,)),
-            pltpu.SemaphoreType.DMA((PARTS * 14,)),
-            pltpu.SemaphoreType.DMA((PARTS * 14,)),
-            pltpu.SemaphoreType.DMA((PARTS * 16,)),
-            pltpu.SemaphoreType.DMA((PARTS * 16,)),
+            pltpu.SemaphoreType.DMA((PARTS,)),
+            pltpu.SemaphoreType.DMA((PARTS * MOVES,)),
+            pltpu.SemaphoreType.DMA((PARTS,)),
             pltpu.SemaphoreType.DMA((PARTS * 2,)),
             pltpu.SemaphoreType.DMA((PARTS * 2,)),
+            pltpu.SemaphoreType.DMA((PARTS * 2,)),
+            pltpu.SemaphoreType.DMA((PARTS,)),
             pltpu.SemaphoreType.DMA((PARTS,)),
         ],
         compiler_params=pltpu.CompilerParams(

time: 96.6 us -> 93.8 us (0.971)
  Pallas kernels: 93.9 us -> 91.1 us
    pallas_call x1, Pallas kernels: 93.9 us -> 91.1 us  [per_device(): pl.pallas_call(kernel, out_shape=jax.ShapeDtypeStruct((ROWS, COLS), BF16)...]
where the time goes in v4:
time: 93.8 us; the launch traced here: 93.6 us
  Pallas kernels  91.1 us (97%)
  local copies, waits for them, and re-layouts  1.87 us (2%)
    pallas_call x1, Pallas kernels, per_device(): pl.pallas_call(kernel, out_shape=jax.ShapeDtypeStruct((ROWS, COLS), BF16)...  91.1 us

profile of v4, /device:TPU:1, one launch (start us, length us, event | category | flops | bytes accessed | tf_op | source)
XLA Modules:
  0.0 93.6 jit_solution(2782858811018009450)
XLA Ops:
  0.7 91.1 %shard_map.73 = bf16[512,512]{1,0:T(8,128)(2,1)} custom-call(bf16[2048,128]{1,0:T(8,128)(2,1)} %bitcast.3, bf16[2048,128]{1,0:T(8,128)(2,1)} %bitcast.4, s32[1,2048]{1,0:T(1,128)} %sensor_ref.1, s32[1,2048]{1,0:T(1,128)} %window_ref.1, s32[1,2048]{1,0:T(1,128)} %bitcast.5, s32[1,1]{1,0:T(1,128)S(6)} %copy.9.count_ref, bf16[1024,512]{1,0:T(8,128)(2,1)} %cal_ref.1), custom_call_target="tpu_custom_call" | custom-call | tf_op jit(solution)/shard_map/pallas_call | solution.py:646
  91.7 1.9 %copy.10 = bf16[512,512]{1,0:T(8,128)(2,1)} copy(bf16[512,512]{1,0:T(8,128)(2,1)} %shard_map.73) | data formatting | bytes 1048576

commit v5 on v4

--- a/solution.py
+++ b/solution.py
@@ -538,34 +538,35 @@
     place(xm, 1)
     below(1, 3)
     send_up(1, 4).start()
-    below(1, 2)
     above(0, 3)
     send_down(0, 4).start()
-    above(1, 2)
+    x_copy(xp, 0, 4, right).wait_recv()
+    x_copy(xp, 1, 5, right).wait_recv()
+    prepare(xp)
+    send_across(3, 0).start()
+    place(xp, 0)
     above(1, 3)
     send_down(1, 4).start()
     below(2, 0)
     send_up(2, 2).start()
     send_across(2, 4).start()
+    send_up(3, 1).start()
+    send_down(3, 1).start()
+    send_across(3, 1).start()
+    below(1, 2)
+    above(1, 2)
     beside(0, 3)
     beside(0, 2)
-    x_copy(xp, 0, 4, right).wait_recv()
-    x_copy(xp, 1, 5, right).wait_recv()
-    prepare(xp)
-    send_across(3, 0).start()
-    place(xp, 0)
     beside(1, 2)
     beside(1, 3)
     place(xp, 1)
     beside(2, 5)
     send_down(2, 4).start()
-    send_across(3, 1).start()
     x_copy(xo, 0, 8, left).wait_recv()
     x_copy(xo, 1, 9, left).wait_recv()
     x_copy(xo, 2, 10, right).wait_recv()
     x_copy(xo, 3, 11, right).wait_recv()
     prepare(xo)
-    send_up(3, 1).start()
     place(xo, 0)
     beside(2, 4)
     send_up(2, 4).start()
@@ -581,33 +582,32 @@
     above(2, 1)
     send_across(2, 3).start()
     above(2, 2)
-    send_down(3, 1).start()
     place(xo, 1)
     beside(3, 1)
     send_down(3, 3).start()
     below(1, 4)
     below(2, 2)
     above(0, 4)
-    above(1, 4)
     early(0)
-    late(0)
-    above(2, 4)
-    early(1)
     below(3, 1)
     send_across(3, 2).start()
+    above(3, 1)
+    send_across(3, 3).start()
+    above(1, 4)
+    late(0)
+    early(1)
     late(1)
+    below(3, 3)
+    send_up(3, 4).start()
+    above(3, 3)
+    send_down(3, 4).start()
+    above(2, 4)
     beside(2, 3)
     beside(2, 2)
+    below(2, 4)
     early(2)
-    above(3, 1)
-    send_across(3, 3).start()
     above(3, 2)
-    above(3, 3)
-    send_down(3, 4).start()
     below(3, 2)
-    below(3, 3)
-    send_up(3, 4).start()
-    below(2, 4)
     late(2)
     beside(3, 2)
     beside(3, 3)
@@ -615,6 +615,7 @@
     above(3, 4)
     early(3)
     late(3)
+
     def sent(ref, sem):
         pltpu.make_async_copy(ref, ref, sem).wait()
 

time: 93.8 us -> 93.3 us (level)
  no operation moved by 1% of the time
where the time goes in v5:
time: 93.3 us; the launch traced here: 93.1 us
  Pallas kernels  90.5 us (97%)
  local copies, waits for them, and re-layouts  1.87 us (2%)
    pallas_call x1, Pallas kernels, per_device(): pl.pallas_call(kernel, out_shape=jax.ShapeDtypeStruct((ROWS, COLS), BF16)...  90.5 us
    unnamed x1, local copies, waits for them, and re-layouts  1.87 us

profile of v5, /device:TPU:1, one launch (start us, length us, event | category | flops | bytes accessed | tf_op | source)
XLA Modules:
  0.0 93.1 jit_solution(12905833234206921346)
XLA Ops:
  0.7 90.5 %shard_map.73 = bf16[512,512]{1,0:T(8,128)(2,1)} custom-call(bf16[2048,128]{1,0:T(8,128)(2,1)} %bitcast.3, bf16[2048,128]{1,0:T(8,128)(2,1)} %bitcast.4, s32[1,2048]{1,0:T(1,128)} %sensor_ref.1, s32[1,2048]{1,0:T(1,128)} %window_ref.1, s32[1,2048]{1,0:T(1,128)} %bitcast.5, s32[1,1]{1,0:T(1,128)S(6)} %copy.9.count_ref, bf16[1024,512]{1,0:T(8,128)(2,1)} %cal_ref.1), custom_call_target="tpu_custom_call" | custom-call | tf_op jit(solution)/shard_map/pallas_call | solution.py:647
  91.2 1.9 %copy.10 = bf16[512,512]{1,0:T(8,128)(2,1)} copy(bf16[512,512]{1,0:T(8,128)(2,1)} %shard_map.73) | data formatting | bytes 1048576
